TPU v7x, 256 devices: a whole 4x4x8 slice. The times are simulated.
256 devices in a mesh: seq: 32 (over y, x, core), head: 8 (over z).
Axes of the slice: x: 4, y: 4, z: 8, core: 2. Of those that a mesh axis runs over, the one named last changes fastest.
Arguments:
- queries: bfloat16 [4096, 64, 128], P('seq', 'head'), may hold values from -150 to 150
- key_store: bfloat16 [4096, 8, 128], P(('seq', 'head')), may hold values from -5.2 to 5.2
- value_store: bfloat16 [4096, 8, 128], P(('seq', 'head')), may hold values from -6 to 6
- upstream: bfloat16 [4096, 64, 128], P('seq', 'head'), may hold values from -5 to 5
- fork_pages: int32 [32, 8], P('seq'), may hold values from 0 to 31, as said below
- fork_visible: int32 [32, 8], P('seq'), may hold values from 1 to 128
Outputs:
- attended: bfloat16 [4096, 64, 128], P('seq', 'head')
- query_grad: bfloat16 [4096, 64, 128], P('seq', 'head')
- key_grad: bfloat16 [4096, 8, 128], P(('seq', 'head'))
- value_grad: bfloat16 [4096, 8, 128], P(('seq', 'head'))
Inputs may be any that keep to these rules, and one draw needn't show every extreme that they name: `fork_pages`: page p is held by seq index p. The 8 entries of the blocks of one seq index never name its own pages; at most 2 of them name pages held by any one other seq index, and exactly 2 name pages held by some one other seq index.
All inputs are finite; a program needn't handle non-finite values.
Results may differ from a plain program's by a relative error of at most 0.019.
Values may be sent and summed in bfloat16 or wider, within the bound.
A program may use at most 64 MiB of HBM per device.

v0:
```python
import math

import jax
import jax.numpy as jnp
from jax import lax
from jax.sharding import PartitionSpec as P

HD = 128
BLK = 128
FORKS = 8


HIGH = lax.Precision.HIGHEST


def side_by_side(arrays, axis, split_dim, concat_dim, along):
    widths = [a.shape[along] for a in arrays]
    both = jnp.concatenate(arrays, axis=along)
    out = lax.all_to_all(both, axis, split_axis=split_dim, concat_axis=concat_dim, tiled=True)
    return tuple(jnp.split(out, [sum(widths[:k]) for k in range(1, len(widths))], axis=along))


def sent_together(arrays, axis, dim, along):
    both = jnp.concatenate(arrays, axis=along)
    out, at, finished = (lax.all_gather(both, axis, axis=dim, tiled=True), 0, [])
    for a in arrays:
        finished.append(lax.slice_in_dim(out, at, at + a.shape[along], axis=along))
        at += a.shape[along]
    return tuple(finished)


def attend_block(query_blk, grad_blk, key_cat, value_cat, fork_limit):
    row_total, head_total, head_dim = query_blk.shape
    kv_total = key_cat.shape[1]
    groups = head_total // kv_total
    factor = 1.0 / math.sqrt(head_dim)
    query_grid = query_blk.reshape(row_total, kv_total, groups, head_dim)
    grad_grid = grad_blk.reshape(row_total, kv_total, groups, head_dim)
    scores = (
        jnp.einsum("qkgd,skd->kgqs", query_grid, key_cat, preferred_element_type=jnp.float32)
        * factor
    )
    positions = jnp.arange(row_total, dtype=jnp.int32)
    causal = positions[None, :] <= positions[:, None]
    fork_part = (positions[None, :] < fork_limit[:, None]).reshape(-1)
    allowed = jnp.concatenate(
        [causal, jnp.broadcast_to(fork_part[None, :], (row_total, fork_part.shape[0]))], axis=1
    )
    scores = jnp.where(allowed, scores, -1e30)
    row_max = jnp.max(scores, axis=-1, keepdims=True)
    exp_scores = jnp.where(allowed, jnp.exp(scores - row_max), 0.0)
    weights = exp_scores / jnp.sum(exp_scores, axis=-1, keepdims=True)
    weights_b = weights.astype(jnp.bfloat16)
    attended = jnp.einsum(
        "kgqs,skd->qkgd", weights_b, value_cat, preferred_element_type=jnp.float32
    ).astype(jnp.bfloat16)
    row_delta = jnp.sum(grad_grid.astype(jnp.float32) * attended.astype(jnp.float32), axis=-1)
    weight_grad = jnp.einsum(
        "qkgd,skd->kgqs", grad_grid, value_cat, preferred_element_type=jnp.float32
    )
    score_grad = (weights * (weight_grad - jnp.transpose(row_delta, (1, 2, 0))[..., None])).astype(
        jnp.bfloat16
    )
    query_grad = (
        jnp.einsum("kgqs,skd->qkgd", score_grad, key_cat, preferred_element_type=jnp.float32)
        * factor
    ).astype(jnp.bfloat16)
    key_grad = (
        jnp.einsum("kgqs,qkgd->skd", score_grad, query_grid, preferred_element_type=jnp.float32)
        * factor
    )
    value_grad = jnp.einsum(
        "kgqs,qkgd->skd", weights_b, grad_grid, preferred_element_type=jnp.float32
    )
    return (
        attended.reshape(row_total, head_total, head_dim),
        query_grad.reshape(row_total, head_total, head_dim),
        key_grad,
        value_grad,
    )


def per_device(queries, key_store, value_store, upstream, fork_pages, fork_visible):
    local_keys, local_values = side_by_side((key_store, value_store), "head", 1, 0, 2)
    local_heads = local_keys.shape[1]
    row_width = local_heads * HD
    page_count = fork_pages.shape[0]
    fork_flat = fork_pages.reshape(-1)
    entries = fork_flat.shape[0]
    blank = jnp.zeros((entries, BLK, row_width), jnp.bfloat16)
    shard_pair = sent_together((local_keys, local_values), "seq", 0, 1)
    shard_keys = shard_pair[0].reshape(-1, BLK, row_width)
    shard_values = shard_pair[1].reshape(-1, BLK, row_width)
    held_pages = shard_keys.shape[0]
    inside = (fork_flat >= 0) & (fork_flat < held_pages)
    position = jnp.clip(fork_flat, 0, held_pages - 1)
    new_keys = jnp.where(inside[:, None, None], jnp.take(shard_keys, position, axis=0), blank)
    new_values = jnp.where(inside[:, None, None], jnp.take(shard_values, position, axis=0), blank)
    fork_keys = new_keys.reshape(page_count, FORKS, BLK, local_heads, HD)
    fork_values = new_values.reshape(page_count, FORKS, BLK, local_heads, HD)
    query_blocks = queries.reshape(page_count, BLK, queries.shape[1], HD)
    grad_blocks = upstream.reshape(page_count, BLK, queries.shape[1], HD)
    self_keys = local_keys.reshape(page_count, BLK, local_heads, HD)
    self_values = local_values.reshape(page_count, BLK, local_heads, HD)

    def run_block(block_items):
        query_blk, grad_blk, own_key, own_value, ancestor_keys, ancestor_values, fork_limit = (
            block_items
        )
        key_cat = jnp.concatenate([own_key[None], ancestor_keys], 0).reshape(-1, local_heads, HD)
        value_cat = jnp.concatenate([own_value[None], ancestor_values], 0).reshape(
            -1, local_heads, HD
        )
        return attend_block(query_blk, grad_blk, key_cat, value_cat, fork_limit)

    attended, query_grad, key_grad, value_grad = lax.map(
        run_block,
        (query_blocks, grad_blocks, self_keys, self_values, fork_keys, fork_values, fork_visible),
    )
    key_grad = key_grad.reshape(page_count, FORKS + 1, BLK, row_width)
    value_grad = value_grad.reshape(page_count, FORKS + 1, BLK, row_width)
    own_key_grad = key_grad[:, 0]
    own_value_grad = value_grad[:, 0]
    fork_key_grad = key_grad[:, 1:].reshape(entries, BLK, row_width)
    fork_value_grad = value_grad[:, 1:].reshape(entries, BLK, row_width)
    stacked = jnp.concatenate(
        [fork_key_grad.reshape(entries, -1), fork_value_grad.reshape(entries, -1)], axis=1
    )
    targets = jnp.arange(lax.axis_size("seq") * page_count, dtype=jnp.int32)
    chooser = (fork_flat[None, :] == targets[:, None]).astype(jnp.float32)
    summed = lax.psum_scatter(
        jnp.dot(chooser, stacked, precision=HIGH), "seq", scatter_dimension=0, tiled=True
    )
    key_part = BLK * row_width
    own_key_grad = own_key_grad + summed[:, :key_part].reshape(own_key_grad.shape)
    own_value_grad = own_value_grad + summed[:, key_part:].reshape(own_value_grad.shape)
    key_rounded = own_key_grad.astype(jnp.bfloat16).reshape(page_count * BLK, local_heads, HD)
    value_rounded = own_value_grad.astype(jnp.bfloat16).reshape(page_count * BLK, local_heads, HD)
    key_out, value_out = side_by_side((key_rounded, value_rounded), "head", 0, 1, 2)
    return (attended.reshape(queries.shape), query_grad.reshape(queries.shape), key_out, value_out)


def solution(mesh):
    placed = (
        P("seq", "head", None),
        P(("seq", "head"), None, None),
        P(("seq", "head"), None, None),
        P("seq", "head", None),
        P("seq", None),
        P("seq", None),
    )
    return jax.shard_map(
        per_device,
        mesh=mesh,
        in_specs=placed,
        out_specs=(
            P("seq", "head", None),
            P("seq", "head", None),
            P(("seq", "head"), None, None),
            P(("seq", "head"), None, None),
        ),
        check_vma=False,
    )
```

profile of v0, /device:TPU:1, one launch (start us, length us, event | category | flops | bytes accessed | tf_op | source)
XLA Modules:
  0.0 235.2 jit_solution(17395849488417490264)
XLA Ops:
  7.2 0.8 copy.40
  8.0 0.8 copy.41
  8.8 16.0 %all_to_all.36 = bf16[16,8,256]{2,0,1:T(8,128)(2,1)S(1)} all-to-all(bf16[16,8,256]{2,0,1:T(8,128)(2,1)S(1)} %pad_maximum_fusion.3), channel_id=1, replica_groups=mesh['seq'=32,'head'=8] {'head'}, dimensions={1} | all-to-all | bytes 131072 | tf_op jit(solution)/shard_map/all_to_all | solution.py:19
  24.9 0.6 pad_maximum_fusion.4
  25.6 1.2 copy.48
  26.7 0.7 fusion.31
  27.5 0.7 compare_and_fusion
  28.4 44.1 %all-gather.2.cloned.1.call-done = bf16[4096,2,128]{2,0,1:T(8,128)(2,1)} async-done(((bf16[128,2,128]{2,0,1:T(8,128)(2,1)}), bf16[4096,2,128]{2,0,1:T(8,128)(2,1)}) %all-gather.2.cloned.1.call-update) | async-done | bytes 2097168 | tf_op jit(solution)/shard_map/all_gather | solution.py:25
  72.4 1.7 fusion.35
  74.1 0.6 gather_fusion.1
  74.7 0.6 gather_fusion
  75.5 0.8 fusion.2
  76.4 1.0 fusion.4
  77.4 1.2 fusion.7
  78.6 2.1 fusion.21
  80.7 1.6 fusion.5
  82.4 0.8 fusion.6
  83.9 3.7 %fusion.17 = f32[32,32768]{1,0:T(8,128)} fusion(f32[8,16384]{1,0:T(8,128)S(1)} %bitcast.167, f32[8,16384]{1,0:T(8,128)S(1)} %bitcast.168, s32[8]{0:T(128)S(1)} %bitcast.180), kind=kOutput, calls=%fused_computation.23 | convolution fusion | flops 100925696 | bytes 5242912 | tf_op jit(solution)/shard_map/dot_general | solution.py:132
  87.7 0.6 dynamic-slice.4
  88.3 1.5 slice.41
  89.8 0.6 slice.38
  90.4 118.1 %all-reduce.3.cloned.1.call-done = f32[32,32768]{1,0:T(8,128)} async-done(((f32[32,32768]{1,0:T(8,128)}), f32[32,32768]{1,0:T(8,128)}) %all-reduce.3.cloned.1.call-update) | async-done | bytes 4194320
  208.5 2.1 fusion.28
  211.3 1.0 reduce.3
  212.3 0.6 reshape.258
  212.9 6.7 %all-to-all-start.1 = ((bf16[8,2,2048]{2,1,0:T(2,128)(2,1)}), bf16[8,2,2048]{2,1,0:T(2,128)(2,1)S(1)}, u32[]{:S(2)}, u32[]{:S(2)}) async-start(bf16[8,2,2048]{2,1,0:T(2,128)(2,1)} %reshape.258), calls=%async_computation.1 | async-start | bytes 131072 | tf_op jit(solution)/shard_map/all_to_all | solution.py:19
  219.7 0.5 fusion.16
  220.2 1.8 copy.55
  222.1 0.9 copy.56
  222.9 4.1 %all-to-all-done.1 = bf16[8,2,2048]{2,1,0:T(2,128)(2,1)S(1)} async-done(((bf16[8,2,2048]{2,1,0:T(2,128)(2,1)}), bf16[8,2,2048]{2,1,0:T(2,128)(2,1)S(1)}, u32[]{:S(2)}, u32[]{:S(2)}) %all-to-all-start.1) | async-done | bytes 65568 | tf_op jit(solution)/shard_map/all_to_all | solution.py:19
  227.1 0.6 copy.58
  227.7 0.6 copy.57
  (29 shorter events, 2.0 us)
Async XLA Ops:
  7.2 68.4 %copy-start = (bf16[128,8,128]{2,1,0:T(8,128)(2,1)S(1)}, bf16[128,8,128]{2,1,0:T(8,128)(2,1)}, u32[]{:S(2)}) copy-start(bf16[128,8,128]{2,1,0:T(8,128)(2,1)} %param.8) | copy-start | bytes 786436
  7.2 65.3 %all-gather.2.cloned.1.call-start = ((), (), s32[]{:S(2)}) async-start(), calls=%async_computation.2 | async-start | bytes 2162688 | tf_op jit(solution)/shard_map/all_gather | solution.py:25
  25.5 183.0 %all-reduce.3.cloned.1.call-start = ((), (), s32[]{:S(2)}) async-start(), calls=%async_computation.3 | async-start | bytes 8388608
  78.6 4.6 %copy-start.1 = (f32[1152,128,1]{1,0,2:T(8,128)}, f32[1152,128,1]{1,0,2:T(8,128)S(1)}, u32[]{:S(2)}) copy-start(f32[1152,128,1]{1,0,2:T(8,128)S(1)} %fusion.7) | copy-start | bytes 1769476
  82.4 1.5 copy-start.2
  83.9 3.8 %copy-start.3 = (u32[256]{0:T(256)S(1)}, u32[256]{0:T(256)}, u32[]{:S(2)}) copy-start(u32[256]{0:T(256)} %constant.62) | copy-start | bytes 3076
  212.9 14.0 %all-to-all-start.1 = ((bf16[8,2,2048]{2,1,0:T(2,128)(2,1)}), bf16[8,2,2048]{2,1,0:T(2,128)(2,1)S(1)}, u32[]{:S(2)}, u32[]{:S(2)}) async-start(bf16[8,2,2048]{2,1,0:T(2,128)(2,1)} %reshape.258), calls=%async_computation.1 | async-start | bytes 131072 | tf_op jit(solution)/shard_map/all_to_all | solution.py:19
Sparse Core Ops, SparseCore 0:
  25.6 46.7 all-gather.1
  87.8 120.6 all-reduce.2
where the time goes:
time: 237 us; the launch traced here: 235 us
  waiting for transfers between devices  166 us (70%)
  blocking collectives  16 us (7%)
  between operations  14.3 us (6%)
  local copies, waits for them, and re-layouts  14.2 us (6%)
  matrix products  10.9 us (5%)
  starting transfers between devices  6.81 us (3%)
  other arithmetic  6.71 us (3%)
    unnamed x3, waiting for transfers between devices  118 us
    all_gather x1, waiting for transfers between devices, sent_together(): lax.all_gather(both, axis, axis=dim, tiled=True)  44.1 us
    all_to_all x1, blocking collectives, side_by_side(): lax.all_to_all(both, axis, split_axis=split_dim, concat_axis=concat_dim,...  16 us
    unnamed x23, local copies, waits for them, and re-layouts  8.69 us
    all_to_all x1, starting transfers between devices, side_by_side(): lax.all_to_all(both, axis, split_axis=split_dim, concat_axis=concat_dim,...  6.73 us
  transfers between devices with their start and end apart: 3, of which 3 were waited for; matrix products, arithmetic and copies ran while one was open for 4% of the time, Pallas kernels for 0%

commit v1 on v0

v1 whole, which is shorter than its diff:
```python
import functools
import math

import jax
import jax.numpy as jnp
from jax import lax
from jax.experimental import pallas as pl
from jax.experimental.pallas import tpu as pltpu
from jax.sharding import PartitionSpec as P

HD = 128
BLK = 128
FORKS = 8
ENT = FORKS + 1
CW = 256
F32 = jnp.float32
BF16 = jnp.bfloat16
MESH = pl.DeviceIdType.MESH
NT = (((1,), (1,)), ((), ()))
FACTOR = 1.0 / math.sqrt(HD)
LOG2E = 1.4426950408889634
NEG = -1e30


def dot(a, b):
    return jnp.dot(a, b, preferred_element_type=F32)


def dot_nt(a, b):
    return lax.dot_general(a, b, NT, preferred_element_type=F32)


def remote(src, dst, send_sem, recv_sem, seq, head):
    return pltpu.make_async_remote_copy(
        src_ref=src, dst_ref=dst, send_sem=send_sem, recv_sem=recv_sem,
        device_id=(seq, head), device_id_type=MESH,
    )


def kernel(
    nx, ny, nz, groups,
    fork_ref, vis_ref, k_ref, v_ref, q_hbm, g_hbm,
    att_hbm, qg_hbm, kg_ref, vg_ref,
    q_buf, g_buf, gt_buf, att_buf, qg_buf, delta_buf,
    zsrc, kpages, vpages, ksel, vsel, kt_sel, vt_sel, s_buf,
    acc, slot_of, dsend, prec, rsend, rrec, fin, zrec,
    io_sem, z_send, z_recv, ag_send, ag_recv, fw_send, fw_recv,
    dd_send, dd_recv, rs_send, rs_recv, zb_send, zb_recv,
):
    nc = nx * ny
    rows = BLK * groups
    chunks = rows // CW
    sub = BLK // nz
    seq = lax.axis_index("seq")
    z = lax.axis_index("head")
    core = lax.rem(seq, 2)
    chip = seq // 2
    x = lax.rem(chip, nx)
    y = chip // nx
    partner = chip * 2 + (1 - core)

    def ring(d, n):
        return min(d, n - d)

    offsets = [(dx, dy) for dy in range(ny) for dx in range(nx)]
    far = sorted(range(1, nc), key=lambda o: -(ring(offsets[o][0], nx) + ring(offsets[o][1], ny)))
    near = far[::-1]

    def chip_at(o, sign):
        dx, dy = offsets[o]
        tx = lax.rem(x + (dx if sign > 0 else nx - dx), nx)
        ty = lax.rem(y + (dy if sign > 0 else ny - dy), ny)
        return ty * nx + tx

    load_q = pltpu.make_async_copy(q_hbm, q_buf, io_sem.at[0])
    load_g = pltpu.make_async_copy(g_hbm, g_buf, io_sem.at[1])
    load_g.start()
    load_q.start()

    barrier = pltpu.get_barrier_semaphore()
    for o in range(1, nz):
        pl.semaphore_signal(barrier, inc=1, device_id=(seq, lax.rem(z + o, nz)), device_id_type=MESH)
    for o in far:
        pl.semaphore_signal(barrier, inc=1, device_id=(chip_at(o, 1) * 2 + core, z), device_id_type=MESH)
    pl.semaphore_signal(barrier, inc=1, device_id=(partner, z), device_id_type=MESH)

    r0 = lax.broadcasted_iota(jnp.int32, (BLK, BLK), 0)
    r1 = lax.broadcasted_iota(jnp.int32, (BLK, BLK), 1)
    to_heads = (r1 == lax.rem(r0, sub) * nz + r0 // sub).astype(BF16)
    to_tokens = (r1 == lax.rem(r0, nz) * sub + r0 // nz).astype(BF16)
    pages = (kpages, vpages)
    for t, ref in enumerate((k_ref, v_ref)):
        zsrc[t] = dot(to_heads, ref[...]).astype(BF16).reshape(nz, sub, HD)
        pages[t][seq, z] = zsrc[t, z]

    pl.semaphore_wait(barrier, nz - 1 + nc - 1 + 1)

    def z_copy(t, o):
        head = lax.rem(z + o, nz)
        return remote(zsrc.at[t, head], pages[t].at[seq, z], z_send.at[t, o], z_recv.at[t, o], seq, head)

    z_order = sorted(range(1, nz), key=lambda o: -ring(o, nz))
    for t in range(2):
        for o in z_order:
            z_copy(t, o).start()

    def entry_slots(p, _):
        first = jnp.int32(ENT)
        second = jnp.int32(ENT)
        for e in range(FORKS):
            hit = fork_ref[0, e] == p
            second = jnp.where(hit & (first < ENT), e + 1, second)
            first = jnp.where(hit & (first == ENT), e + 1, first)
        slot_of[0, p] = first
        slot_of[1, p] = second
        return 0

    lax.fori_loop(0, 2 * nc, entry_slots, 0)
    acc[0, ENT] = jnp.zeros((BLK, HD), F32)
    acc[1, ENT] = jnp.zeros((BLK, HD), F32)

    load_g.wait()
    for c in range(chunks):
        gt_buf[c] = g_buf[c * CW:(c + 1) * CW, :].T

    def z_wait(t):
        for o in z_order[::-1]:
            head = lax.rem(z + nz - o, nz)
            here = pages[t].at[seq, head]
            remote(here, here, z_send.at[t, o], z_recv.at[t, o], seq, head).wait_recv()

    def page_send(t, o):
        ref = pages[t].at[seq]
        return remote(ref, ref, ag_send.at[t, o], ag_recv.at[t, o], chip_at(o, 1) * 2 + core, z)

    def page_forward(t, o):
        ref = pages[t].at[chip_at(o, -1) * 2 + core] if o else pages[t].at[seq]
        return remote(ref, ref, fw_send.at[t, o], fw_recv.at[t, o], partner, z)

    def page_arrival(t, o):
        src = chip_at(o, -1) * 2 + core
        ref = pages[t].at[src]
        return remote(ref, ref, ag_send.at[t, o], ag_recv.at[t, o], src, z)

    def forward_arrival(t, o):
        ref = pages[t].at[chip_at(o, -1) * 2 + (1 - core)] if o else pages[t].at[partner]
        return remote(ref, ref, fw_send.at[t, o], fw_recv.at[t, o], partner, z)

    for t in range(2):
        z_wait(t)
        for o in far:
            page_send(t, o).start()
        page_forward(t, 0).start()

    def collect(t):
        for o in near:
            page_arrival(t, o).wait_recv()
            page_forward(t, o).start()
        for o in [0] + near:
            forward_arrival(t, o).wait_recv()

    def select_pages(t, sel, sel_t):
        for e in range(ENT):
            page = pages[t][seq] if e == 0 else pages[t][fork_ref[0, e - 1]]
            page = page.reshape(BLK, HD)
            sel[e] = page
            sel_t[:, e * BLK:(e + 1) * BLK] = page.T

    collect(0)
    select_pages(0, ksel, kt_sel)
    load_q.wait()

    key_row = lax.broadcasted_iota(jnp.int32, (BLK, CW), 0)
    col = lax.broadcasted_iota(jnp.int32, (BLK, CW), 1)

    def halves(a):
        return a.reshape(BLK // 8, 8, CW)

    def scores(c, _):
        q_c = q_buf[pl.ds(pl.multiple_of(c * CW, CW), CW), :]
        top = jnp.full((8, CW), NEG, F32)
        for e in range(ENT):
            raw = dot_nt(ksel[e], q_c) * (FACTOR * LOG2E)
            if e == 0:
                seen = key_row <= (col + c * CW) // groups
            else:
                seen = key_row < vis_ref[0, e - 1]
            raw = jnp.where(seen, raw, NEG)
            s_buf[c, e] = raw
            top = jnp.maximum(top, jnp.max(halves(raw), axis=0))
        top = jnp.max(top, axis=0, keepdims=True)
        total = jnp.zeros((8, CW), F32)
        for e in range(ENT):
            expo = jnp.exp2(s_buf[c, e] - top)
            s_buf[c, e] = expo
            total = total + jnp.sum(halves(expo), axis=0)
        delta_buf[c] = jnp.broadcast_to(1.0 / jnp.sum(total, axis=0, keepdims=True), (8, CW))
        return 0

    lax.fori_loop(0, chunks, scores, 0)

    collect(1)
    select_pages(1, vsel, vt_sel)

    for e in range(ENT):
        acc[0, e] = jnp.zeros((BLK, HD), F32)
        acc[1, e] = jnp.zeros((BLK, HD), F32)

    def values(c, _):
        rows_c = pl.ds(pl.multiple_of(c * CW, CW), CW)
        g_c = g_buf[rows_c, :]
        inverse = delta_buf[c][:1]
        out_t = jnp.zeros((HD, CW), F32)
        for e in range(ENT):
            w = s_buf[c, e] * inverse
            s_buf[c, e] = w
            w_b = w.astype(BF16)
            out_t = out_t + dot(vt_sel[:, e * BLK:(e + 1) * BLK], w_b)
            acc[1, e] += dot(w_b, g_c)
        out_b = out_t.astype(BF16)
        att_buf[rows_c, :] = out_b.T
        delta = jnp.sum(out_b.astype(F32) * gt_buf[c].astype(F32), axis=0, keepdims=True)
        delta_buf[c] = jnp.broadcast_to(delta, (8, CW))
        return 0

    lax.fori_loop(0, chunks, values, 0)
    store_att = pltpu.make_async_copy(att_buf, att_hbm, io_sem.at[2])
    store_att.start()

    def slot_sum(t, page):
        return acc[t, slot_of[0, page]] + acc[t, slot_of[1, page]]

    def partner_send(t, o):
        return remote(dsend.at[t, o], prec.at[t, o], dd_send.at[t, o], dd_recv.at[t, o], partner, z)

    def reduce_send(t, o):
        return remote(rsend.at[t, o], rrec.at[t, o], rs_send.at[t, o], rs_recv.at[t, o], chip_at(o, 1) * 2 + core, z)

    def to_partner(t):
        for o in far + [0]:
            dsend[t, o] = slot_sum(t, chip_at(o, 1) * 2 + (1 - core)).astype(BF16)
            partner_send(t, o).start()

    def to_chips(t):
        for o in far:
            partner_send(t, o).wait_recv()
            mine = slot_sum(t, chip_at(o, 1) * 2 + core) + prec[t, o].astype(F32)
            rsend[t, o] = mine.astype(BF16)
            reduce_send(t, o).start()
        partner_send(t, 0).wait_recv()

    to_partner(1)
    to_chips(1)

    def grads(c, _):
        rows_c = pl.ds(pl.multiple_of(c * CW, CW), CW)
        g_c = g_buf[rows_c, :]
        q_c = q_buf[rows_c, :]
        delta = delta_buf[c][:1]
        dq_t = jnp.zeros((HD, CW), F32)
        for e in range(ENT):
            ds = (s_buf[c, e] * (dot_nt(vsel[e], g_c) - delta)).astype(BF16)
            dq_t = dq_t + dot(kt_sel[:, e * BLK:(e + 1) * BLK], ds)
            acc[0, e] += dot(ds, q_c)
        qg_buf[rows_c, :] = (dq_t * FACTOR).T.astype(BF16)
        return 0

    lax.fori_loop(0, chunks, grads, 0)
    store_qg = pltpu.make_async_copy(qg_buf, qg_hbm, io_sem.at[3])
    store_qg.start()
    to_partner(0)
    to_chips(0)

    def zb_copy(t, o):
        head = lax.rem(z + o, nz)
        return remote(fin.at[t, head], zrec.at[t, z], zb_send.at[t, o], zb_recv.at[t, o], seq, head)

    def finish(t):
        total = acc[t, 0] + slot_sum(t, seq) + prec[t, 0].astype(F32)
        for o in near:
            reduce_send(t, o).wait_recv()
            total = total + rrec[t, o].astype(F32)
        if t == 0:
            total = total * FACTOR
        fin[t] = total.astype(BF16).reshape(nz, sub, HD)
        zrec[t, z] = fin[t, z]
        for o in z_order:
            zb_copy(t, o).start()

    def result(t, out_ref):
        for o in z_order[::-1]:
            head = lax.rem(z + nz - o, nz)
            here = zrec.at[t, head]
            remote(here, here, zb_send.at[t, o], zb_recv.at[t, o], seq, head).wait_recv()
        out_ref[...] = dot(to_tokens, zrec[t].reshape(BLK, HD)).astype(BF16)

    finish(1)
    finish(0)
    result(1, vg_ref)
    result(0, kg_ref)

    store_att.wait()
    store_qg.wait()
    for t in range(2):
        for o in range(1, nz):
            z_copy(t, o).wait_send()
            zb_copy(t, o).wait_send()
        for o in range(1, nc):
            page_send(t, o).wait_send()
            reduce_send(t, o).wait_send()
        for o in range(nc):
            page_forward(t, o).wait_send()
            partner_send(t, o).wait_send()


def per_device(nx, ny, nz, queries, key_store, value_store, upstream, fork_pages, fork_visible):
    groups = queries.shape[1]
    rows = BLK * groups
    chunks = rows // CW
    nc = nx * ny
    sub = BLK // nz
    dma = pltpu.SemaphoreType.DMA
    smem = pl.BlockSpec(memory_space=pltpu.SMEM)
    vmem = pl.BlockSpec(memory_space=pltpu.VMEM)
    hbm = pl.BlockSpec(memory_space=pl.ANY)
    big = jax.ShapeDtypeStruct((rows, HD), BF16)
    small = jax.ShapeDtypeStruct((BLK, HD), BF16)
    att, qg, kg, vg = pl.pallas_call(
        functools.partial(kernel, nx, ny, nz, groups),
        out_shape=(big, big, small, small),
        in_specs=[smem, smem, vmem, vmem, hbm, hbm],
        out_specs=(hbm, hbm, vmem, vmem),
        scratch_shapes=[
            pltpu.VMEM((rows, HD), BF16),
            pltpu.VMEM((rows, HD), BF16),
            pltpu.VMEM((chunks, HD, CW), BF16),
            pltpu.VMEM((rows, HD), BF16),
            pltpu.VMEM((rows, HD), BF16),
            pltpu.VMEM((chunks, 8, CW), F32),
            pltpu.VMEM((2, nz, sub, HD), BF16),
            pltpu.VMEM((2 * nc, nz, sub, HD), BF16),
            pltpu.VMEM((2 * nc, nz, sub, HD), BF16),
            pltpu.VMEM((ENT, BLK, HD), BF16),
            pltpu.VMEM((ENT, BLK, HD), BF16),
            pltpu.VMEM((HD, ENT * BLK), BF16),
            pltpu.VMEM((HD, ENT * BLK), BF16),
            pltpu.VMEM((chunks, ENT, BLK, CW), F32),
            pltpu.VMEM((2, ENT + 1, BLK, HD), F32),
            pltpu.SMEM((2, 2 * nc), jnp.int32),
            pltpu.VMEM((2, nc, BLK, HD), BF16),
            pltpu.VMEM((2, nc, BLK, HD), BF16),
            pltpu.VMEM((2, nc, BLK, HD), BF16),
            pltpu.VMEM((2, nc, BLK, HD), BF16),
            pltpu.VMEM((2, nz, sub, HD), BF16),
            pltpu.VMEM((2, nz, sub, HD), BF16),
            dma((4,)),
            dma((2, nz)), dma((2, nz)),
            dma((2, nc)), dma((2, nc)),
            dma((2, nc)), dma((2, nc)),
            dma((2, nc)), dma((2, nc)),
            dma((2, nc)), dma((2, nc)),
            dma((2, nz)), dma((2, nz)),
        ],
        compiler_params=pltpu.CompilerParams(collective_id=0, has_side_effects=True),
    )(
        fork_pages, fork_visible,
        key_store.reshape(BLK, HD), value_store.reshape(BLK, HD),
        queries.reshape(rows, HD), upstream.reshape(rows, HD),
    )
    return (
        att.reshape(queries.shape), qg.reshape(queries.shape),
        kg.reshape(key_store.shape), vg.reshape(value_store.shape),
    )


def solution(mesh):
    nc = mesh.shape["seq"] // 2
    nx = 1
    while nx * nx < nc:
        nx *= 2
    placed = (
        P("seq", "head", None),
        P(("seq", "head"), None, None),
        P(("seq", "head"), None, None),
        P("seq", "head", None),
        P("seq", None),
        P("seq", None),
    )
    return jax.shard_map(
        functools.partial(per_device, nx, nc // nx, mesh.shape["head"]),
        mesh=mesh,
        in_specs=placed,
        out_specs=(
            P("seq", "head", None),
            P("seq", "head", None),
            P(("seq", "head"), None, None),
            P(("seq", "head"), None, None),
        ),
        check_vma=False,
    )
```

time: 237 us -> 63.6 us (0.27)
  waiting for transfers between devices: 166 us -> 0 us
  Pallas kernels: 0 us -> 58.8 us
  blocking collectives: 16 us -> 0 us
  between operations: 14.3 us -> 0.65 us
  matrix products: 10.9 us -> 0 us
  local copies, waits for them, and re-layouts: 14.2 us -> 3.86 us
  starting transfers between devices: 6.81 us -> 0 us
  other arithmetic: 6.71 us -> 0 us
    unnamed x3 -> x0, waiting for transfers between devices: 118 us -> none
    pallas_call x0 -> x1, Pallas kernels: none -> 58.8 us  [per_device(): pl.pallas_call(functools.partial(kernel, nx, ny, nz, groups), out_shape=(...]
    all_gather x1 -> x0, waiting for transfers between devices: 44.1 us -> none  [sent_together(): lax.all_gather(both, axis, axis=dim, tiled=True)]
    all_to_all x1 -> x0, blocking collectives: 16 us -> none  [side_by_side(): lax.all_to_all(both, axis, split_axis=split_dim, concat_axis=concat_dim,...]
    dot_general x7 -> x0, matrix products: 10.9 us -> none  [the longest x1 3.74 us: per_device(): jnp.dot(chooser, stacked, precision=HIGH)]
    all_to_all x1 -> x0, starting transfers between devices: 6.73 us -> none  [side_by_side(): lax.all_to_all(both, axis, split_axis=split_dim, concat_axis=concat_dim,...]
    unnamed x23 -> x10, local copies, waits for them, and re-layouts: 8.69 us -> 3.86 us
    all_to_all x1 -> x0, waiting for transfers between devices: 4.06 us -> none  [side_by_side(): lax.all_to_all(both, axis, split_axis=split_dim, concat_axis=concat_dim,...]
  transfers between devices with their start and end apart: 3 -> 0, of which waited for: 3 -> 0; matrix products, arithmetic and copies ran while one was open for 4% -> 0% of each run, Pallas kernels for 0% -> 0%
where the time goes in v1:
time: 63.6 us; the launch traced here: 63.3 us
  Pallas kernels  58.8 us (92%)
  local copies, waits for them, and re-layouts  3.86 us (6%)
  between operations  0.65 us (1%)
    pallas_call x1, Pallas kernels, per_device(): pl.pallas_call(functools.partial(kernel, nx, ny, nz, groups), out_shape=(...  58.8 us
    unnamed x10, local copies, waits for them, and re-layouts  3.86 us

profile of v1, /device:TPU:1, one launch (start us, length us, event | category | flops | bytes accessed | tf_op | source)
XLA Modules:
  0.0 63.3 jit_solution(8993697881469874236)
XLA Ops:
  0.6 58.8 %shard_map.93 = (bf16[1024,128]{1,0:T(8,128)(2,1)}, bf16[1024,128]{1,0:T(8,128)(2,1)}, bf16[128,128]{1,0:T(8,128)(2,1)}, bf16[128,128]{1,0:T(8,128)(2,1)}) custom-call(s32[1,8]{1,0:T(1,128)} %fork_ref.1, s32[1,8]{1,0:T(1,128)} %vis_ref.1, bf16[128,128]{1,0:T(8,128)(2,1)} %bitcast.12, bf16[128,128]{1,0:T(8,128)(2,1)} %bitcast.13, bf16[1024,128]{1,0:T(8,128)(2,1)} %bitcast.8, ...), custom_call_target="tpu_custom_call" | custom-call | tf_op jit(solution)/shard_map/pallas_call | solution.py:328
  59.4 0.0 copy-start
  59.4 1.7 %copy.14 = bf16[128,8,128]{2,1,0:T(8,128)(2,1)} copy(bf16[128,8,128]{2,1,0:T(8,128)(2,1)} %bitcast.11) | data formatting | bytes 524288
  61.1 0.0 copy-done
  61.1 0.0 copy-start.2
  61.1 0.7 %copy.15 = bf16[128,8,128]{2,1,0:T(8,128)(2,1)} copy(bf16[128,8,128]{2,1,0:T(8,128)(2,1)S(1)} %bitcast.10) | data formatting | bytes 524288
  61.8 0.1 copy-done.2
  61.9 0.0 copy-start.1
  61.9 0.6 copy.16
  62.5 0.2 copy-done.1
  62.6 0.6 copy.17
Async XLA Ops:
  59.4 1.7 %copy-start = (bf16[1024,128]{1,0:T(8,128)(2,1)S(1)}, bf16[1024,128]{1,0:T(8,128)(2,1)}, u32[]{:S(2)}) copy-start(bf16[1024,128]{1,0:T(8,128)(2,1)} %get-tuple-element.9) | copy-start | bytes 786436
  61.1 0.8 %copy-start.2 = (bf16[128,128]{1,0:T(8,128)(2,1)S(1)}, bf16[128,128]{1,0:T(8,128)(2,1)}, u32[]{:S(2)}) copy-start(bf16[128,128]{1,0:T(8,128)(2,1)} %get-tuple-element.10) | copy-start | bytes 98308
  61.9 0.8 %copy-start.1 = (bf16[128,128]{1,0:T(8,128)(2,1)S(1)}, bf16[128,128]{1,0:T(8,128)(2,1)}, u32[]{:S(2)}) copy-start(bf16[128,128]{1,0:T(8,128)(2,1)} %get-tuple-element.11) | copy-start | bytes 98308

commit v2 on v1

v2 whole, which is shorter than its diff:
```python
import functools
import math

import jax
import jax.numpy as jnp
from jax import lax
from jax.experimental import pallas as pl
from jax.experimental.pallas import tpu as pltpu
from jax.sharding import PartitionSpec as P

HD = 128
BLK = 128
FORKS = 8
ENT = FORKS + 1
CW = 256
F32 = jnp.float32
BF16 = jnp.bfloat16
MESH = pl.DeviceIdType.MESH
NT = (((1,), (1,)), ((), ()))
FACTOR = 1.0 / math.sqrt(HD)
LOG2E = 1.4426950408889634
NEG = -1e30


def dot(a, b):
    return jnp.dot(a, b, preferred_element_type=F32)


def dot_nt(a, b):
    return lax.dot_general(a, b, NT, preferred_element_type=F32)


def remote(src, dst, send_sem, recv_sem, seq, head):
    return pltpu.make_async_remote_copy(
        src_ref=src, dst_ref=dst, send_sem=send_sem, recv_sem=recv_sem,
        device_id=(seq, head), device_id_type=MESH,
    )


def kernel(
    nx, ny, nz, groups,
    fork_hbm, vis_hbm, k_hbm, v_hbm, q_hbm, g_hbm,
    att_hbm, qg_hbm, kg_ref, vg_ref,
    att_ref, qg_ref, kv_in, q_buf, g_buf, gt_buf, delta_buf,
    zsrc, kpages, vpages, ksel, vsel, kt_sel, vt_sel, s_buf,
    acc, fork_ref, vis_ref, slot_of, dsend, prec, rsend, rrec, ssend, srec, fin, zrec,
    io_sem, z_send, z_recv, ag_send, ag_recv, fw_send, fw_recv,
    dd_send, dd_recv, r1_send, r1_recv, r2_send, r2_recv, zb_send, zb_recv,
):
    nc = nx * ny
    rows = BLK * groups
    chunks = rows // CW
    sub = BLK // nz
    hb = BLK // 2
    hz = nz // 2
    seq = lax.axis_index("seq")
    z = lax.axis_index("head")
    core = lax.rem(seq, 2)
    chip = seq // 2
    x = lax.rem(chip, nx)
    y = chip // nx
    partner = chip * 2 + (1 - core)

    def ring(d, n):
        return min(d, n - d)

    offsets = [(dx, dy) for dy in range(ny) for dx in range(nx)]
    far = sorted(range(1, nc), key=lambda o: -(ring(offsets[o][0], nx) + ring(offsets[o][1], ny)))
    near = far[::-1]
    rel = [(j + 1) // 2 if j % 2 else (nz - j // 2) % nz for j in range(nz)]
    slot_at = {r: j for j, r in enumerate(rel)}
    bounds = [0, 1, 3, 5, 8] if nz == 8 else [0, 1, nz]
    parts = list(zip(bounds[:-1], bounds[1:]))
    part_of = [p for p, (lo, hi) in enumerate(parts) for _ in range(lo, hi)]

    def chip_at(dx, dy):
        return lax.rem(y + dy, ny) * nx + lax.rem(x + dx, nx)

    def chip_to(o):
        return chip_at(*offsets[o])

    def chip_from(o):
        dx, dy = offsets[o]
        return chip_at((nx - dx) % nx, (ny - dy) % ny)

    loads = [
        pltpu.make_async_copy(k_hbm, kv_in.at[0], io_sem.at[0]),
        pltpu.make_async_copy(v_hbm, kv_in.at[1], io_sem.at[1]),
        pltpu.make_async_copy(g_hbm, g_buf, io_sem.at[2]),
        pltpu.make_async_copy(q_hbm, q_buf, io_sem.at[3]),
        pltpu.make_async_copy(fork_hbm, fork_ref, io_sem.at[4]),
        pltpu.make_async_copy(vis_hbm, vis_ref, io_sem.at[5]),
    ]
    barrier = pltpu.get_barrier_semaphore()
    for o in range(1, nz):
        pl.semaphore_signal(barrier, inc=1, device_id=(seq, lax.rem(z + o, nz)), device_id_type=MESH)
    for o in far:
        pl.semaphore_signal(barrier, inc=1, device_id=(chip_to(o) * 2 + core, z), device_id_type=MESH)
    pl.semaphore_signal(barrier, inc=1, device_id=(partner, z), device_id_type=MESH)
    for load in loads:
        load.start()

    r0 = lax.broadcasted_iota(jnp.int32, (BLK, BLK), 0)
    r1 = lax.broadcasted_iota(jnp.int32, (BLK, BLK), 1)

    def slot_head(j):
        return lax.rem(z + jnp.where(lax.rem(j, 2) == 1, (j + 1) // 2, nz - j // 2), nz)

    to_heads = (r1 == lax.rem(r0, sub) * nz + r0 // sub).astype(BF16)
    from_slots = (lax.rem(r0, nz) == slot_head(r1 // sub)) & (r0 // nz == lax.rem(r1, sub))
    from_slots = from_slots.astype(F32).astype(BF16)
    pages = (kpages, vpages)
    for t in range(2):
        loads[t].wait()
        zsrc[t] = dot(to_heads, kv_in[t]).astype(BF16).reshape(nz, sub, HD)
        pages[t][chip, core, 0] = zsrc[t, z]

    pl.semaphore_wait(barrier, nz - 1 + nc - 1 + 1)

    def z_copy(t, o):
        head = lax.rem(z + o, nz)
        dst = pages[t].at[chip, core, slot_at[(nz - o) % nz]]
        return remote(zsrc.at[t, head], dst, z_send.at[0], z_recv.at[t, part_of[slot_at[(nz - o) % nz]]], seq, head)

    def page_part(t, page, part):
        lo, hi = parts[part]
        return pages[t].at[page // 2, lax.rem(page, 2), pl.ds(lo, hi - lo)]

    def page_send(t, part, o):
        ref = page_part(t, seq, part)
        return remote(ref, ref, ag_send.at[t], ag_recv.at[t, part], chip_to(o) * 2 + core, z)

    def page_arrivals(t, part):
        lo, hi = parts[part]
        ref = pages[t].at[pl.ds(0, nc - 1), 0, pl.ds(lo, hi - lo)]
        return remote(ref, ref, ag_send.at[t], ag_recv.at[t, part], partner, z)

    def page_forward(t, part):
        lo, hi = parts[part]
        ref = pages[t].at[pl.ds(0, nc), core, pl.ds(lo, hi - lo)]
        return remote(ref, ref, fw_send.at[t], fw_recv.at[t, part], partner, z)

    z_order = sorted(range(1, nz), key=lambda o: -ring(o, nz))
    for o in z_order:
        for t in range(2):
            z_copy(t, o).start()

    def send_part(part):
        lo, hi = parts[part]
        for t in range(2):
            if part:
                here = pages[t].at[chip, core, pl.ds(lo, hi - lo)]
                remote(here, here, z_send.at[0], z_recv.at[t, part], seq, lax.rem(z + 1, nz)).wait_recv()
            for o in far:
                page_send(t, part, o).start()

    send_part(0)

    def entry_slots(p, _):
        first = jnp.int32(ENT)
        second = jnp.int32(ENT)
        for e in range(FORKS):
            hit = fork_ref[0, e] == p
            second = jnp.where(hit & (first < ENT), e + 1, second)
            first = jnp.where(hit & (first == ENT), e + 1, first)
        slot_of[0, p] = first
        slot_of[1, p] = second
        return 0

    loads[2].wait()
    for c in range(chunks):
        gt_buf[c] = g_buf[c * CW:(c + 1) * CW, :].T

    for part in range(1, len(parts)):
        send_part(part)
    loads[4].wait()
    lax.fori_loop(0, 2 * nc, entry_slots, 0)
    for t in range(2):
        for e in range(ENT + 1):
            acc[t, e] = jnp.zeros((BLK, HD), F32)

    def collect(t, part):
        page_arrivals(t, part).wait_recv()
        page_forward(t, part).start()

    def collected(t):
        for part in range(len(parts)):
            page_forward(t, part).wait_recv()

    def select_pages(t, sel, sel_t):
        for e in range(ENT):
            page = pages[t][chip, core] if e == 0 else pages[t][fork_ref[0, e - 1] // 2, lax.rem(fork_ref[0, e - 1], 2)]
            page = page.reshape(BLK, HD)
            sel[e] = page
            sel_t[:, e * BLK:(e + 1) * BLK] = page.T

    last = len(parts) - 1
    for part in range(last):
        collect(0, part)
        collect(1, part)
    collect(0, last)
    collected(0)
    select_pages(0, ksel, kt_sel)
    loads[3].wait()
    loads[5].wait()

    slot_row = lax.broadcasted_iota(jnp.int32, (BLK, CW), 0)
    key_row = slot_head(slot_row // sub) * sub + lax.rem(slot_row, sub)
    col = lax.broadcasted_iota(jnp.int32, (BLK, CW), 1)

    def halves(a):
        return a.reshape(BLK // 8, 8, CW)

    def scores(c, _):
        q_c = q_buf[pl.ds(pl.multiple_of(c * CW, CW), CW), :]
        top = jnp.full((8, CW), NEG, F32)
        for e in range(ENT):
            raw = dot_nt(ksel[e], q_c) * (FACTOR * LOG2E)
            if e == 0:
                seen = key_row <= (col + c * CW) // groups
            else:
                seen = key_row < vis_ref[0, e - 1]
            raw = jnp.where(seen, raw, NEG)
            s_buf[c, e] = raw
            top = jnp.maximum(top, jnp.max(halves(raw), axis=0))
        top = jnp.max(top, axis=0, keepdims=True)
        total = jnp.zeros((8, CW), F32)
        for e in range(ENT):
            expo = jnp.exp2(s_buf[c, e] - top)
            s_buf[c, e] = expo
            total = total + jnp.sum(halves(expo), axis=0)
        delta_buf[c] = jnp.broadcast_to(1.0 / jnp.sum(total, axis=0, keepdims=True), (8, CW))
        return 0

    lax.fori_loop(0, chunks, scores, 0)

    collect(1, last)
    collected(1)
    select_pages(1, vsel, vt_sel)

    def values(c, _):
        rows_c = pl.ds(pl.multiple_of(c * CW, CW), CW)
        g_c = g_buf[rows_c, :]
        inverse = delta_buf[c][:1]
        out_t = jnp.zeros((HD, CW), F32)
        for e in range(ENT):
            w = s_buf[c, e] * inverse
            s_buf[c, e] = w
            w_b = w.astype(BF16)
            out_t = out_t + dot(vt_sel[:, e * BLK:(e + 1) * BLK], w_b)
            acc[1, e] += dot(w_b, g_c)
        out_b = out_t.astype(BF16)
        att_ref[rows_c, :] = out_b.T
        delta = jnp.sum(out_b.astype(F32) * gt_buf[c].astype(F32), axis=0, keepdims=True)
        delta_buf[c] = jnp.broadcast_to(delta, (8, CW))
        return 0

    lax.fori_loop(0, chunks, values, 0)
    store_att = pltpu.make_async_copy(att_ref, att_hbm, io_sem.at[6])
    store_att.start()

    def spot(t, h, a, b):
        dx, dy = (a, b) if (t + h) % 2 == 0 else (b, a)
        return chip_at(dx, dy)

    def size_a(t, h):
        return nx if (t + h) % 2 == 0 else ny

    def size_b(t, h):
        return ny if (t + h) % 2 == 0 else nx

    def far_first(n):
        return sorted(range(1, n), key=lambda d: -ring(d, n))

    def slot_sum(t, h, page):
        part = pl.ds(h * hb, hb)
        return acc[t, slot_of[0, page], part] + acc[t, slot_of[1, page], part]

    def partner_send(t, h, a):
        return remote(dsend.at[t, h, a], prec.at[t, h, a], dd_send.at[0], dd_recv.at[t, h, a], partner, z)

    def first_send(t, h, a):
        to = spot(t, h, a, 0) * 2 + core
        return remote(rsend.at[t, h, a], rrec.at[t, h, a], r1_send.at[0], r1_recv.at[t, h], to, z)

    def second_send(t, h, b):
        to = spot(t, h, 0, b) * 2 + core
        return remote(ssend.at[t, h, b], srec.at[t, h, b], r2_send.at[0], r2_recv.at[t, h], to, z)

    def to_partner(t):
        for h in (1, 0):
            for a in far_first(size_a(t, h)) + [0]:
                for b in range(size_b(t, h)):
                    dsend[t, h, a, b] = slot_sum(t, h, spot(t, h, a, b) * 2 + (1 - core)).astype(BF16)
                partner_send(t, h, a).start()

    def mine(t, h, a, b):
        return slot_sum(t, h, spot(t, h, a, b) * 2 + core) + prec[t, h, a, b].astype(F32)

    def first_step(t, h):
        for a in far_first(size_a(t, h)):
            partner_send(t, h, a).wait_recv()
            for b in range(size_b(t, h)):
                rsend[t, h, a, b] = mine(t, h, a, b).astype(BF16)
            first_send(t, h, a).start()

    def gathered(t, h, b):
        total = mine(t, h, 0, b)
        for a in range(1, size_a(t, h)):
            total = total + rrec[t, h, a, b].astype(F32)
        return total

    def second_step(t, h):
        partner_send(t, h, 0).wait_recv()
        here = rrec.at[t, h, pl.ds(1, size_a(t, h) - 1)]
        remote(here, here, r1_send.at[0], r1_recv.at[t, h], partner, z).wait_recv()
        for b in far_first(size_b(t, h)):
            ssend[t, h, b] = gathered(t, h, b).astype(BF16)
            second_send(t, h, b).start()

    def zb_copy(t, j):
        back = slot_at[(nz - rel[j]) % nz]
        return remote(fin.at[t, j], zrec.at[t, back], zb_send.at[0], zb_recv.at[t], seq, lax.rem(z + rel[j], nz))

    def finish(t, h):
        total = acc[t, 0, h * hb:(h + 1) * hb] + gathered(t, h, 0)
        here = srec.at[t, h, pl.ds(1, size_b(t, h) - 1)]
        remote(here, here, r2_send.at[0], r2_recv.at[t, h], partner, z).wait_recv()
        for b in range(1, size_b(t, h)):
            total = total + srec[t, h, b].astype(F32)
        if t == 0:
            total = total * FACTOR
        fin[t, h * hz:(h + 1) * hz] = total.astype(BF16).reshape(hz, sub, HD)
        for j in range((h + 1) * hz - 1, h * hz - 1, -1):
            if j == 0:
                zrec[t, 0] = fin[t, 0]
            else:
                zb_copy(t, j).start()

    def result(t, out_ref):
        here = zrec.at[t, pl.ds(1, nz - 1)]
        remote(here, here, zb_send.at[0], zb_recv.at[t], seq, lax.rem(z + 1, nz)).wait_recv()
        out_ref[...] = dot(from_slots, zrec[t].reshape(BLK, HD)).astype(BF16)

    def grads(c, _):
        rows_c = pl.ds(pl.multiple_of(c * CW, CW), CW)
        g_c = g_buf[rows_c, :]
        q_c = q_buf[rows_c, :]
        delta = delta_buf[c][:1]
        dq_t = jnp.zeros((HD, CW), F32)
        for e in range(ENT):
            ds = (s_buf[c, e] * (dot_nt(vsel[e], g_c) - delta)).astype(BF16)
            dq_t = dq_t + dot(kt_sel[:, e * BLK:(e + 1) * BLK], ds)
            acc[0, e] += dot(ds, q_c)
        qg_ref[rows_c, :] = (dq_t * FACTOR).T.astype(BF16)
        return 0

    to_partner(1)
    lax.fori_loop(0, chunks // 2, grads, 0)
    first_step(1, 1)
    first_step(1, 0)
    lax.fori_loop(chunks // 2, chunks, grads, 0)
    store_qg = pltpu.make_async_copy(qg_ref, qg_hbm, io_sem.at[7])
    store_qg.start()
    to_partner(0)
    second_step(1, 1)
    second_step(1, 0)
    first_step(0, 1)
    first_step(0, 0)
    finish(1, 1)
    finish(1, 0)
    second_step(0, 1)
    second_step(0, 0)
    finish(0, 1)
    finish(0, 0)
    result(1, vg_ref)
    result(0, kg_ref)

    store_att.wait()
    store_qg.wait()
    def sent(ref, sem):
        remote(ref, ref, sem, r2_recv.at[0, 0], partner, z).wait_send()

    sent(zsrc.at[:, pl.ds(1, nz - 1)], z_send.at[0])
    sent(dsend, dd_send.at[0])
    sent(rsend.at[:, :, pl.ds(1, nx - 1)], r1_send.at[0])
    sent(ssend.at[:, :, pl.ds(1, nx - 1)], r2_send.at[0])
    sent(fin.at[:, pl.ds(1, nz - 1)], zb_send.at[0])
    for t in range(2):
        sent(pages[t].at[pl.ds(0, nc - 1), 0], ag_send.at[t])
        sent(pages[t].at[:, 0], fw_send.at[t])


def emit(*refs):
    n = (len(refs) - 2) // 3
    sems_in, sems_out = refs[-2:]
    reads = [pltpu.make_async_copy(refs[i], refs[2 * n + i], sems_in.at[i]) for i in range(n)]
    writes = [pltpu.make_async_copy(refs[2 * n + i], refs[n + i], sems_out.at[i]) for i in range(n)]
    for read in reads:
        read.start()
    for read, write in zip(reads, writes):
        read.wait()
        write.start()
    for write in writes:
        write.wait()


def per_device(nx, ny, nz, queries, key_store, value_store, upstream, fork_pages, fork_visible):
    groups = queries.shape[1]
    rows = BLK * groups
    chunks = rows // CW
    nc = nx * ny
    sub = BLK // nz
    hb = BLK // 2
    nm = max(nx, ny)
    dma = pltpu.SemaphoreType.DMA
    vmem = pl.BlockSpec(memory_space=pltpu.VMEM)
    hbm = pl.BlockSpec(memory_space=pltpu.HBM)
    big = jax.ShapeDtypeStruct((rows, HD), BF16)
    small = jax.ShapeDtypeStruct((BLK, HD), BF16)
    outs = (big, big, small, small)
    results = pl.pallas_call(
        functools.partial(kernel, nx, ny, nz, groups),
        out_shape=outs,
        in_specs=[hbm] * 6,
        out_specs=(hbm, hbm, vmem, vmem),
        scratch_shapes=[
            pltpu.VMEM((rows, HD), BF16),
            pltpu.VMEM((rows, HD), BF16),
            pltpu.VMEM((2, BLK, HD), BF16),
            pltpu.VMEM((rows, HD), BF16),
            pltpu.VMEM((rows, HD), BF16),
            pltpu.VMEM((chunks, HD, CW), BF16),
            pltpu.VMEM((chunks, 8, CW), F32),
            pltpu.VMEM((2, nz, sub, HD), BF16),
            pltpu.VMEM((nc, 2, nz, sub, HD), BF16),
            pltpu.VMEM((nc, 2, nz, sub, HD), BF16),
            pltpu.VMEM((ENT, BLK, HD), BF16),
            pltpu.VMEM((ENT, BLK, HD), BF16),
            pltpu.VMEM((HD, ENT * BLK), BF16),
            pltpu.VMEM((HD, ENT * BLK), BF16),
            pltpu.VMEM((chunks, ENT, BLK, CW), F32),
            pltpu.VMEM((2, ENT + 1, BLK, HD), F32),
            pltpu.SMEM((1, FORKS), jnp.int32),
            pltpu.SMEM((1, FORKS), jnp.int32),
            pltpu.SMEM((2, 2 * nc), jnp.int32),
            pltpu.VMEM((2, 2, nm, nm, hb, HD), BF16),
            pltpu.VMEM((2, 2, nm, nm, hb, HD), BF16),
            pltpu.VMEM((2, 2, nm, nm, hb, HD), BF16),
            pltpu.VMEM((2, 2, nm, nm, hb, HD), BF16),
            pltpu.VMEM((2, 2, nm, hb, HD), BF16),
            pltpu.VMEM((2, 2, nm, hb, HD), BF16),
            pltpu.VMEM((2, nz, sub, HD), BF16),
            pltpu.VMEM((2, nz, sub, HD), BF16),
            dma((8,)),
            dma((1,)), dma((2, 4)),
            dma((2,)), dma((2, 4)),
            dma((2,)), dma((2, 4)),
            dma((1,)), dma((2, 2, nm)),
            dma((1,)), dma((2, 2)),
            dma((1,)), dma((2, 2)),
            dma((1,)), dma((2,)),
        ],
        compiler_params=pltpu.CompilerParams(
            collective_id=0, has_side_effects=True
        ),
    )(
        fork_pages, fork_visible,
        key_store.reshape(BLK, HD), value_store.reshape(BLK, HD),
        queries.reshape(rows, HD), upstream.reshape(rows, HD),
    )
    att, qg, kg, vg = pl.pallas_call(
        emit,
        out_shape=outs,
        in_specs=[hbm] * 4,
        out_specs=(hbm,) * 4,
        scratch_shapes=[pltpu.VMEM(o.shape, BF16) for o in outs] + [dma((4,)), dma((4,))],
    )(*results)
    return (
        att.reshape(queries.shape), qg.reshape(queries.shape),
        kg.reshape(key_store.shape), vg.reshape(value_store.shape),
    )


def solution(mesh):
    nc = mesh.shape["seq"] // 2
    nx = 1
    while nx * nx < nc:
        nx *= 2
    placed = (
        P("seq", "head", None),
        P(("seq", "head"), None, None),
        P(("seq", "head"), None, None),
        P("seq", "head", None),
        P("seq", None),
        P("seq", None),
    )
    return jax.shard_map(
        functools.partial(per_device, nx, nc // nx, mesh.shape["head"]),
        mesh=mesh,
        in_specs=placed,
        out_specs=(
            P("seq", "head", None),
            P("seq", "head", None),
            P(("seq", "head"), None, None),
            P(("seq", "head"), None, None),
        ),
        check_vma=False,
    )
```

time: 63.6 us -> 56.4 us (0.89)
  local copies, waits for them, and re-layouts: 3.86 us -> 0 us
  Pallas kernels: 58.8 us -> 55.7 us
    unnamed x10 -> x0, local copies, waits for them, and re-layouts: 3.86 us -> none
    pallas_call x1 -> x2, Pallas kernels: 58.8 us -> 55.7 us  [the longest x1 53.8 us: per_device(): pl.pallas_call(functools.partial(kernel, nx, ny, nz, groups), out_shape=o...]
where the time goes in v2:
time: 56.4 us; the launch traced here: 56.3 us
  Pallas kernels  55.7 us (99%)
  between operations  0.64 us (1%)
    pallas_call x1, Pallas kernels, per_device(): pl.pallas_call(functools.partial(kernel, nx, ny, nz, groups), out_shape=o...  53.8 us
    pallas_call x1, Pallas kernels, per_device(): pl.pallas_call(emit, out_shape=outs, in_specs=[hbm] * 4, out_specs=(hbm,)...  1.82 us

profile of v2, /device:TPU:1, one launch (start us, length us, event | category | flops | bytes accessed | tf_op | source)
XLA Modules:
  0.0 56.3 jit_solution(2246509176895067143)
XLA Ops:
  0.6 53.8 %shard_map.93 = (bf16[1024,128]{1,0:T(8,128)(2,1)}, bf16[1024,128]{1,0:T(8,128)(2,1)}, bf16[128,128]{1,0:T(8,128)(2,1)}, bf16[128,128]{1,0:T(8,128)(2,1)}) custom-call(s32[1,8]{1,0:T(1,128)} %fork_hbm.1, s32[1,8]{1,0:T(1,128)} %vis_hbm.1, bf16[128,128]{1,0:T(8,128)(2,1)} %bitcast.10, bf16[128,128]{1,0:T(8,128)(2,1)} %bitcast.11, bf16[1024,128]{1,0:T(8,128)(2,1)} %bitcast.8, ...), custom_call_target="tpu_custom_call" | custom-call | tf_op jit(solution)/shard_map/pallas_call | solution.py:422
  54.5 1.8 %shard_map.94 = (bf16[1024,128]{1,0:T(8,128)(2,1)}, bf16[1024,128]{1,0:T(8,128)(2,1)}, bf16[128,128]{1,0:T(8,128)(2,1)}, bf16[128,128]{1,0:T(8,128)(2,1)}) custom-call(bf16[1024,128]{1,0:T(8,128)(2,1)} %get-tuple-element.12.refs_0_, bf16[1024,128]{1,0:T(8,128)(2,1)} %get-tuple-element.13.refs_1_, bf16[128,128]{1,0:T(8,128)(2,1)} %get-tuple-element.14.refs_2_, ...), custom_call_target="tpu_custom_call" | custom-call | tf_op jit(solution)/shard_map/pallas_call | solution.py:472

commit v3 on v2

--- a/solution.py
+++ b/solution.py
@@ -40,11 +40,11 @@
 def kernel(
     nx, ny, nz, groups,
     fork_hbm, vis_hbm, k_hbm, v_hbm, q_hbm, g_hbm,
-    att_hbm, qg_hbm, kg_ref, vg_ref,
-    att_ref, qg_ref, kv_in, q_buf, g_buf, gt_buf, delta_buf,
-    zsrc, kpages, vpages, ksel, vsel, kt_sel, vt_sel, s_buf,
+    att_ref, qg_ref, kg_ref, vg_ref,
+    kv_in, q_buf, g_buf, gt_buf, delta_buf,
+    zsrc, kpages, vpages, ksel, vsel, kt_sel, vt_sel, s_buf, ds_buf,
     acc, fork_ref, vis_ref, slot_of, dsend, prec, rsend, rrec, ssend, srec, fin, zrec,
-    io_sem, z_send, z_recv, ag_send, ag_recv, fw_send, fw_recv,
+    io_sem, z_send, z_recv, la_send, la_recv, pa_send, pa_recv, fw_send, fw_recv,
     dd_send, dd_recv, r1_send, r1_recv, r2_send, r2_recv, zb_send, zb_recv,
 ):
     nc = nx * ny
@@ -64,9 +64,9 @@
     def ring(d, n):
         return min(d, n - d)
 
-    offsets = [(dx, dy) for dy in range(ny) for dx in range(nx)]
-    far = sorted(range(1, nc), key=lambda o: -(ring(offsets[o][0], nx) + ring(offsets[o][1], ny)))
-    near = far[::-1]
+    def far_first(n):
+        return sorted(range(1, n), key=lambda d: -ring(d, n))
+
     rel = [(j + 1) // 2 if j % 2 else (nz - j // 2) % nz for j in range(nz)]
     slot_at = {r: j for j, r in enumerate(rel)}
     bounds = [0, 1, 3, 5, 8] if nz == 8 else [0, 1, nz]
@@ -75,13 +75,6 @@
 
     def chip_at(dx, dy):
         return lax.rem(y + dy, ny) * nx + lax.rem(x + dx, nx)
-
-    def chip_to(o):
-        return chip_at(*offsets[o])
-
-    def chip_from(o):
-        dx, dy = offsets[o]
-        return chip_at((nx - dx) % nx, (ny - dy) % ny)
 
     loads = [
         pltpu.make_async_copy(k_hbm, kv_in.at[0], io_sem.at[0]),
@@ -94,8 +87,10 @@
     barrier = pltpu.get_barrier_semaphore()
     for o in range(1, nz):
         pl.semaphore_signal(barrier, inc=1, device_id=(seq, lax.rem(z + o, nz)), device_id_type=MESH)
-    for o in far:
-        pl.semaphore_signal(barrier, inc=1, device_id=(chip_to(o) * 2 + core, z), device_id_type=MESH)
+    for d in far_first(nx):
+        pl.semaphore_signal(barrier, inc=1, device_id=(chip_at(d, 0) * 2 + core, z), device_id_type=MESH)
+    for d in far_first(ny):
+        pl.semaphore_signal(barrier, inc=1, device_id=(chip_at(0, d) * 2 + core, z), device_id_type=MESH)
     pl.semaphore_signal(barrier, inc=1, device_id=(partner, z), device_id_type=MESH)
     for load in loads:
         load.start()
@@ -113,31 +108,56 @@
     for t in range(2):
         loads[t].wait()
         zsrc[t] = dot(to_heads, kv_in[t]).astype(BF16).reshape(nz, sub, HD)
-        pages[t][chip, core, 0] = zsrc[t, z]
-
-    pl.semaphore_wait(barrier, nz - 1 + nc - 1 + 1)
+        pages[t][y, x, core, 0] = zsrc[t, z]
+
+    pl.semaphore_wait(barrier, nz - 1 + nx - 1 + ny - 1 + 1)
 
     def z_copy(t, o):
         head = lax.rem(z + o, nz)
-        dst = pages[t].at[chip, core, slot_at[(nz - o) % nz]]
+        dst = pages[t].at[y, x, core, slot_at[(nz - o) % nz]]
         return remote(zsrc.at[t, head], dst, z_send.at[0], z_recv.at[t, part_of[slot_at[(nz - o) % nz]]], seq, head)
 
-    def page_part(t, page, part):
+    def x_first(t, k):
+        return (t + k) % 2 == 0
+
+    def spot(t, k, a, b):
+        return chip_at(a, b) if x_first(t, k) else chip_at(b, a)
+
+    def size_a(t, k):
+        return nx if x_first(t, k) else ny
+
+    def size_b(t, k):
+        return ny if x_first(t, k) else nx
+
+    def own_part(t, part):
         lo, hi = parts[part]
-        return pages[t].at[page // 2, lax.rem(page, 2), pl.ds(lo, hi - lo)]
-
-    def page_send(t, part, o):
-        ref = page_part(t, seq, part)
-        return remote(ref, ref, ag_send.at[t], ag_recv.at[t, part], chip_to(o) * 2 + core, z)
-
-    def page_arrivals(t, part):
+        return pages[t].at[y, x, core, pl.ds(lo, hi - lo)]
+
+    def line_send(t, part, d):
+        ref = own_part(t, part)
+        return remote(ref, ref, la_send.at[t], la_recv.at[t, part], spot(t, part, d, 0) * 2 + core, z)
+
+    def line_arrivals(t, part):
         lo, hi = parts[part]
-        ref = pages[t].at[pl.ds(0, nc - 1), 0, pl.ds(lo, hi - lo)]
-        return remote(ref, ref, ag_send.at[t], ag_recv.at[t, part], partner, z)
+        ref = pages[t].at[0, pl.ds(0, size_a(t, part) - 1), 0, pl.ds(lo, hi - lo)]
+        return remote(ref, ref, la_send.at[t], la_recv.at[t, part], partner, z)
+
+    def plane_send(t, part, d):
+        lo, hi = parts[part]
+        if x_first(t, part):
+            ref = pages[t].at[y, pl.ds(0, nx), core, pl.ds(lo, hi - lo)]
+        else:
+            ref = pages[t].at[pl.ds(0, ny), x, core, pl.ds(lo, hi - lo)]
+        return remote(ref, ref, pa_send.at[t], pa_recv.at[t, part], spot(t, part, 0, d) * 2 + core, z)
+
+    def plane_arrivals(t, part):
+        lo, hi = parts[part]
+        ref = pages[t].at[pl.ds(0, ny - 1), pl.ds(0, nx), 0, pl.ds(lo, hi - lo)]
+        return remote(ref, ref, pa_send.at[t], pa_recv.at[t, part], partner, z)
 
     def page_forward(t, part):
         lo, hi = parts[part]
-        ref = pages[t].at[pl.ds(0, nc), core, pl.ds(lo, hi - lo)]
+        ref = pages[t].at[pl.ds(0, ny), pl.ds(0, nx), core, pl.ds(lo, hi - lo)]
         return remote(ref, ref, fw_send.at[t], fw_recv.at[t, part], partner, z)
 
     z_order = sorted(range(1, nz), key=lambda o: -ring(o, nz))
@@ -146,13 +166,18 @@
             z_copy(t, o).start()
 
     def send_part(part):
-        lo, hi = parts[part]
         for t in range(2):
             if part:
-                here = pages[t].at[chip, core, pl.ds(lo, hi - lo)]
+                here = own_part(t, part)
                 remote(here, here, z_send.at[0], z_recv.at[t, part], seq, lax.rem(z + 1, nz)).wait_recv()
-            for o in far:
-                page_send(t, part, o).start()
+            for d in far_first(size_a(t, part)):
+                line_send(t, part, d).start()
+
+    def relay(part):
+        for t in range(2):
+            line_arrivals(t, part).wait_recv()
+            for d in far_first(size_b(t, part)):
+                plane_send(t, part, d).start()
 
     send_part(0)
 
@@ -173,6 +198,10 @@
 
     for part in range(1, len(parts)):
         send_part(part)
+        if part > 1:
+            relay(part - 2)
+    for part in range(max(0, len(parts) - 2), len(parts)):
+        relay(part)
     loads[4].wait()
     lax.fori_loop(0, 2 * nc, entry_slots, 0)
     for t in range(2):
@@ -180,16 +209,19 @@
             acc[t, e] = jnp.zeros((BLK, HD), F32)
 
     def collect(t, part):
-        page_arrivals(t, part).wait_recv()
+        plane_arrivals(t, part).wait_recv()
         page_forward(t, part).start()
 
     def collected(t):
         for part in range(len(parts)):
             page_forward(t, part).wait_recv()
 
+    def page_at(p):
+        return p // (2 * nx), lax.rem(p // 2, nx), lax.rem(p, 2)
+
     def select_pages(t, sel, sel_t):
         for e in range(ENT):
-            page = pages[t][chip, core] if e == 0 else pages[t][fork_ref[0, e - 1] // 2, lax.rem(fork_ref[0, e - 1], 2)]
+            page = pages[t][y, x, core] if e == 0 else pages[t][page_at(fork_ref[0, e - 1])]
             page = page.reshape(BLK, HD)
             sel[e] = page
             sel_t[:, e * BLK:(e + 1) * BLK] = page.T
@@ -256,21 +288,6 @@
         return 0
 
     lax.fori_loop(0, chunks, values, 0)
-    store_att = pltpu.make_async_copy(att_ref, att_hbm, io_sem.at[6])
-    store_att.start()
-
-    def spot(t, h, a, b):
-        dx, dy = (a, b) if (t + h) % 2 == 0 else (b, a)
-        return chip_at(dx, dy)
-
-    def size_a(t, h):
-        return nx if (t + h) % 2 == 0 else ny
-
-    def size_b(t, h):
-        return ny if (t + h) % 2 == 0 else nx
-
-    def far_first(n):
-        return sorted(range(1, n), key=lambda d: -ring(d, n))
 
     def slot_sum(t, h, page):
         part = pl.ds(h * hb, hb)
@@ -347,11 +364,15 @@
         g_c = g_buf[rows_c, :]
         q_c = q_buf[rows_c, :]
         delta = delta_buf[c][:1]
-        dq_t = jnp.zeros((HD, CW), F32)
         for e in range(ENT):
             ds = (s_buf[c, e] * (dot_nt(vsel[e], g_c) - delta)).astype(BF16)
-            dq_t = dq_t + dot(kt_sel[:, e * BLK:(e + 1) * BLK], ds)
+            ds_buf[c, e * BLK:(e + 1) * BLK, :] = ds
             acc[0, e] += dot(ds, q_c)
+        return 0
+
+    def query_grads(c, _):
+        rows_c = pl.ds(pl.multiple_of(c * CW, CW), CW)
+        dq_t = dot(kt_sel[...], ds_buf[c])
         qg_ref[rows_c, :] = (dq_t * FACTOR).T.astype(BF16)
         return 0
 
@@ -360,9 +381,8 @@
     first_step(1, 1)
     first_step(1, 0)
     lax.fori_loop(chunks // 2, chunks, grads, 0)
-    store_qg = pltpu.make_async_copy(qg_ref, qg_hbm, io_sem.at[7])
-    store_qg.start()
     to_partner(0)
+    lax.fori_loop(0, chunks, query_grads, 0)
     second_step(1, 1)
     second_step(1, 0)
     first_step(0, 1)
@@ -376,8 +396,7 @@
     result(1, vg_ref)
     result(0, kg_ref)
 
-    store_att.wait()
-    store_qg.wait()
+
     def sent(ref, sem):
         remote(ref, ref, sem, r2_recv.at[0, 0], partner, z).wait_send()
 
@@ -387,22 +406,18 @@
     sent(ssend.at[:, :, pl.ds(1, nx - 1)], r2_send.at[0])
     sent(fin.at[:, pl.ds(1, nz - 1)], zb_send.at[0])
     for t in range(2):
-        sent(pages[t].at[pl.ds(0, nc - 1), 0], ag_send.at[t])
-        sent(pages[t].at[:, 0], fw_send.at[t])
+        sent(pages[t].at[0, pl.ds(0, nx - 1), 0], la_send.at[t])
+        sent(pages[t].at[pl.ds(0, ny - 1), :, 0], pa_send.at[t])
+        sent(pages[t].at[:, :, 0], fw_send.at[t])
 
 
 def emit(*refs):
-    n = (len(refs) - 2) // 3
-    sems_in, sems_out = refs[-2:]
-    reads = [pltpu.make_async_copy(refs[i], refs[2 * n + i], sems_in.at[i]) for i in range(n)]
-    writes = [pltpu.make_async_copy(refs[2 * n + i], refs[n + i], sems_out.at[i]) for i in range(n)]
-    for read in reads:
-        read.start()
-    for read, write in zip(reads, writes):
-        read.wait()
-        write.start()
-    for write in writes:
-        write.wait()
+    n = (len(refs) - 1) // 2
+    copies = [pltpu.make_async_copy(refs[i], refs[n + i], refs[-1].at[i]) for i in range(n)]
+    for copy in copies:
+        copy.start()
+    for copy in copies:
+        copy.wait()
 
 
 def per_device(nx, ny, nz, queries, key_store, value_store, upstream, fork_pages, fork_visible):
@@ -421,25 +436,24 @@
     outs = (big, big, small, small)
     results = pl.pallas_call(
         functools.partial(kernel, nx, ny, nz, groups),
-        out_shape=outs,
+        out_shape=tuple(pltpu.VMEM(o.shape, BF16) for o in outs),
         in_specs=[hbm] * 6,
-        out_specs=(hbm, hbm, vmem, vmem),
+        out_specs=(vmem,) * 4,
         scratch_shapes=[
-            pltpu.VMEM((rows, HD), BF16),
-            pltpu.VMEM((rows, HD), BF16),
             pltpu.VMEM((2, BLK, HD), BF16),
             pltpu.VMEM((rows, HD), BF16),
             pltpu.VMEM((rows, HD), BF16),
             pltpu.VMEM((chunks, HD, CW), BF16),
             pltpu.VMEM((chunks, 8, CW), F32),
             pltpu.VMEM((2, nz, sub, HD), BF16),
-            pltpu.VMEM((nc, 2, nz, sub, HD), BF16),
-            pltpu.VMEM((nc, 2, nz, sub, HD), BF16),
+            pltpu.VMEM((ny, nx, 2, nz, sub, HD), BF16),
+            pltpu.VMEM((ny, nx, 2, nz, sub, HD), BF16),
             pltpu.VMEM((ENT, BLK, HD), BF16),
             pltpu.VMEM((ENT, BLK, HD), BF16),
             pltpu.VMEM((HD, ENT * BLK), BF16),
             pltpu.VMEM((HD, ENT * BLK), BF16),
             pltpu.VMEM((chunks, ENT, BLK, CW), F32),
+            pltpu.VMEM((chunks, ENT * BLK, CW), BF16),
             pltpu.VMEM((2, ENT + 1, BLK, HD), F32),
             pltpu.SMEM((1, FORKS), jnp.int32),
             pltpu.SMEM((1, FORKS), jnp.int32),
@@ -452,8 +466,9 @@
             pltpu.VMEM((2, 2, nm, hb, HD), BF16),
             pltpu.VMEM((2, nz, sub, HD), BF16),
             pltpu.VMEM((2, nz, sub, HD), BF16),
-            dma((8,)),
+            dma((6,)),
             dma((1,)), dma((2, 4)),
+            dma((2,)), dma((2, 4)),
             dma((2,)), dma((2, 4)),
             dma((2,)), dma((2, 4)),
             dma((1,)), dma((2, 2, nm)),
@@ -472,9 +487,10 @@
     att, qg, kg, vg = pl.pallas_call(
         emit,
         out_shape=outs,
-        in_specs=[hbm] * 4,
+        in_specs=[vmem] * 4,
         out_specs=(hbm,) * 4,
-        scratch_shapes=[pltpu.VMEM(o.shape, BF16) for o in outs] + [dma((4,)), dma((4,))],
+        scratch_shapes=[dma((4,))],
+        compiler_params=pltpu.CompilerParams(vmem_limit_bytes=4 * 2**20),
     )(*results)
     return (
         att.reshape(queries.shape), qg.reshape(queries.shape),

time: 56.4 us -> 51.5 us (0.913)
  Pallas kernels: 55.7 us -> 50.4 us
    pallas_call x2, Pallas kernels: 55.7 us -> 50.4 us  [the longest x1 49.6 us: per_device(): pl.pallas_call(functools.partial(kernel, nx, ny, nz, groups), out_shape=t...]
where the time goes in v3:
time: 51.5 us; the launch traced here: 51.1 us
  Pallas kernels  50.4 us (98%)
  between operations  0.64 us (1%)
    pallas_call x1, Pallas kernels, per_device(): pl.pallas_call(functools.partial(kernel, nx, ny, nz, groups), out_shape=t...  49.6 us

profile of v3, /device:TPU:1, one launch (start us, length us, event | category | flops | bytes accessed | tf_op | source)
XLA Modules:
  0.0 51.1 jit_solution(6389094806110336858)
XLA Ops:
  0.6 49.6 %shard_map.93 = (bf16[1024,128]{1,0:T(8,128)(2,1)S(1)}, bf16[1024,128]{1,0:T(8,128)(2,1)S(1)}, bf16[128,128]{1,0:T(8,128)(2,1)S(1)}, bf16[128,128]{1,0:T(8,128)(2,1)S(1)}) custom-call(s32[1,8]{1,0:T(1,128)} %fork_hbm.1, s32[1,8]{1,0:T(1,128)} %vis_hbm.1, bf16[128,128]{1,0:T(8,128)(2,1)} %bitcast.10, bf16[128,128]{1,0:T(8,128)(2,1)} %bitcast.11, ...), custom_call_target="tpu_custom_call" | custom-call | tf_op jit(solution)/shard_map/pallas_call | solution.py:437
  50.2 0.8 %shard_map.94 = (bf16[1024,128]{1,0:T(8,128)(2,1)}, bf16[1024,128]{1,0:T(8,128)(2,1)}, bf16[128,128]{1,0:T(8,128)(2,1)}, bf16[128,128]{1,0:T(8,128)(2,1)}) custom-call(bf16[1024,128]{1,0:T(8,128)(2,1)S(1)} %get-tuple-element.12.refs_0_, bf16[1024,128]{1,0:T(8,128)(2,1)S(1)} %get-tuple-element.13.refs_1_, bf16[128,128]{1,0:T(8,128)(2,1)S(1)} %get-tuple-element.14.refs_2_, ...), custom_call_target="tpu_custom_call" | custom-call | tf_op jit(solution)/shard_map/pallas_call | solution.py:487

commit v4 on v3

--- a/solution.py
+++ b/solution.py
@@ -41,8 +41,8 @@
     nx, ny, nz, groups,
     fork_hbm, vis_hbm, k_hbm, v_hbm, q_hbm, g_hbm,
     att_ref, qg_ref, kg_ref, vg_ref,
-    kv_in, q_buf, g_buf, gt_buf, delta_buf,
-    zsrc, kpages, vpages, ksel, vsel, kt_sel, vt_sel, s_buf, ds_buf,
+    kv_in, q_buf, g_buf, gt_buf, delta_buf, top_buf, sum_buf,
+    zsrc, knear, kfar, vnear, vfar, ksel, vsel, kt_sel, vt_sel, s_buf, ds_buf,
     acc, fork_ref, vis_ref, slot_of, dsend, prec, rsend, rrec, ssend, srec, fin, zrec,
     io_sem, z_send, z_recv, la_send, la_recv, pa_send, pa_recv, fw_send, fw_recv,
     dd_send, dd_recv, r1_send, r1_recv, r2_send, r2_recv, zb_send, zb_recv,
@@ -69,7 +69,7 @@
 
     rel = [(j + 1) // 2 if j % 2 else (nz - j // 2) % nz for j in range(nz)]
     slot_at = {r: j for j, r in enumerate(rel)}
-    bounds = [0, 1, 3, 5, 8] if nz == 8 else [0, 1, nz]
+    bounds = [0, 1, 3, 4, 5, 8] if nz == 8 else [0, 1, nz]
     parts = list(zip(bounds[:-1], bounds[1:]))
     part_of = [p for p, (lo, hi) in enumerate(parts) for _ in range(lo, hi)]
 
@@ -104,18 +104,19 @@
     to_heads = (r1 == lax.rem(r0, sub) * nz + r0 // sub).astype(BF16)
     from_slots = (lax.rem(r0, nz) == slot_head(r1 // sub)) & (r0 // nz == lax.rem(r1, sub))
     from_slots = from_slots.astype(F32).astype(BF16)
-    pages = (kpages, vpages)
+    pages = ((knear, kfar), (vnear, vfar))
     for t in range(2):
         loads[t].wait()
         zsrc[t] = dot(to_heads, kv_in[t]).astype(BF16).reshape(nz, sub, HD)
-        pages[t][y, x, core, 0] = zsrc[t, z]
+        pages[t][0][y, x, core, 0] = zsrc[t, z]
 
     pl.semaphore_wait(barrier, nz - 1 + nx - 1 + ny - 1 + 1)
 
     def z_copy(t, o):
         head = lax.rem(z + o, nz)
-        dst = pages[t].at[y, x, core, slot_at[(nz - o) % nz]]
-        return remote(zsrc.at[t, head], dst, z_send.at[0], z_recv.at[t, part_of[slot_at[(nz - o) % nz]]], seq, head)
+        j = slot_at[(nz - o) % nz]
+        dst = pages[t][j // hz].at[y, x, core, j % hz]
+        return remote(zsrc.at[t, head], dst, z_send.at[0], z_recv.at[t, part_of[j]], seq, head)
 
     def x_first(t, k):
         return (t + k) % 2 == 0
@@ -129,35 +130,34 @@
     def size_b(t, k):
         return ny if x_first(t, k) else nx
 
+    def part_of_pages(t, part, ys, xs, cs):
+        lo, hi = parts[part]
+        return pages[t][lo // hz].at[ys, xs, cs, pl.ds(lo % hz, hi - lo)]
+
     def own_part(t, part):
-        lo, hi = parts[part]
-        return pages[t].at[y, x, core, pl.ds(lo, hi - lo)]
+        return part_of_pages(t, part, y, x, core)
 
     def line_send(t, part, d):
         ref = own_part(t, part)
         return remote(ref, ref, la_send.at[t], la_recv.at[t, part], spot(t, part, d, 0) * 2 + core, z)
 
     def line_arrivals(t, part):
-        lo, hi = parts[part]
-        ref = pages[t].at[0, pl.ds(0, size_a(t, part) - 1), 0, pl.ds(lo, hi - lo)]
+        ref = part_of_pages(t, part, 0, pl.ds(0, size_a(t, part) - 1), 0)
         return remote(ref, ref, la_send.at[t], la_recv.at[t, part], partner, z)
 
     def plane_send(t, part, d):
-        lo, hi = parts[part]
         if x_first(t, part):
-            ref = pages[t].at[y, pl.ds(0, nx), core, pl.ds(lo, hi - lo)]
+            ref = part_of_pages(t, part, y, pl.ds(0, nx), core)
         else:
-            ref = pages[t].at[pl.ds(0, ny), x, core, pl.ds(lo, hi - lo)]
+            ref = part_of_pages(t, part, pl.ds(0, ny), x, core)
         return remote(ref, ref, pa_send.at[t], pa_recv.at[t, part], spot(t, part, 0, d) * 2 + core, z)
 
     def plane_arrivals(t, part):
-        lo, hi = parts[part]
-        ref = pages[t].at[pl.ds(0, ny - 1), pl.ds(0, nx), 0, pl.ds(lo, hi - lo)]
+        ref = part_of_pages(t, part, pl.ds(0, ny - 1), pl.ds(0, nx), 0)
         return remote(ref, ref, pa_send.at[t], pa_recv.at[t, part], partner, z)
 
     def page_forward(t, part):
-        lo, hi = parts[part]
-        ref = pages[t].at[pl.ds(0, ny), pl.ds(0, nx), core, pl.ds(lo, hi - lo)]
+        ref = part_of_pages(t, part, pl.ds(0, ny), pl.ds(0, nx), core)
         return remote(ref, ref, fw_send.at[t], fw_recv.at[t, part], partner, z)
 
     z_order = sorted(range(1, nz), key=lambda o: -ring(o, nz))
@@ -205,84 +205,107 @@
     loads[4].wait()
     lax.fori_loop(0, 2 * nc, entry_slots, 0)
     for t in range(2):
-        for e in range(ENT + 1):
-            acc[t, e] = jnp.zeros((BLK, HD), F32)
+        for h in range(2):
+            acc[t, h] = jnp.zeros((ENT + 1, hb, HD), F32)
 
     def collect(t, part):
         plane_arrivals(t, part).wait_recv()
         page_forward(t, part).start()
 
-    def collected(t):
-        for part in range(len(parts)):
+    def collected(t, which):
+        for part in which:
             page_forward(t, part).wait_recv()
 
     def page_at(p):
         return p // (2 * nx), lax.rem(p // 2, nx), lax.rem(p, 2)
 
-    def select_pages(t, sel, sel_t):
+    def select_pages(t, sel, h):
         for e in range(ENT):
-            page = pages[t][y, x, core] if e == 0 else pages[t][page_at(fork_ref[0, e - 1])]
-            page = page.reshape(BLK, HD)
-            sel[e] = page
-            sel_t[:, e * BLK:(e + 1) * BLK] = page.T
-
-    last = len(parts) - 1
-    for part in range(last):
+            at = (y, x, core) if e == 0 else page_at(fork_ref[0, e - 1])
+            page = pages[t][h][at[0], at[1], at[2]]
+            sel[h, e * hb:(e + 1) * hb, :] = page.reshape(hb, HD)
+
+    def transposed(sel, sel_t, h):
+        for e in range(ENT):
+            sel_t[h, :, e * hb:(e + 1) * hb] = sel[h, e * hb:(e + 1) * hb, :].T
+
+    slot_row = lax.broadcasted_iota(jnp.int32, (hb, CW), 0)
+    col = lax.broadcasted_iota(jnp.int32, (hb, CW), 1)
+
+    def eights(a):
+        return a.reshape(hb // 8, 8, CW)
+
+    def lanes(c):
+        return pl.ds(pl.multiple_of(c * CW, CW), CW)
+
+    def scores(h):
+        key_row = slot_head(h * hz + slot_row // sub) * sub + lax.rem(slot_row, sub)
+
+        def step(c, _):
+            q_c = q_buf[lanes(c), :]
+            top = jnp.full((8, CW), NEG, F32)
+            for e in range(ENT):
+                raw = dot_nt(ksel[h, e * hb:(e + 1) * hb, :], q_c) * (FACTOR * LOG2E)
+                if e == 0:
+                    seen = key_row <= (col + c * CW) // groups
+                else:
+                    seen = key_row < vis_ref[0, e - 1]
+                raw = jnp.where(seen, raw, NEG)
+                s_buf[c, h, e] = raw
+                top = jnp.maximum(top, jnp.max(eights(raw), axis=0))
+            top = jnp.broadcast_to(jnp.max(top, axis=0, keepdims=True), (8, CW))
+            total = jnp.zeros((8, CW), F32)
+            for e in range(ENT):
+                expo = jnp.exp2(s_buf[c, h, e] - top[:1])
+                s_buf[c, h, e] = expo
+                total = total + jnp.sum(eights(expo), axis=0)
+            top_buf[c, h] = top
+            sum_buf[c, h] = jnp.broadcast_to(jnp.sum(total, axis=0, keepdims=True), (8, CW))
+            return 0
+
+        lax.fori_loop(0, chunks, step, 0)
+
+    near = range(part_of[hz])
+    rest = range(part_of[hz], len(parts))
+    for part in near:
         collect(0, part)
         collect(1, part)
-    collect(0, last)
-    collected(0)
-    select_pages(0, ksel, kt_sel)
+    collected(0, near)
+    select_pages(0, ksel, 0)
     loads[3].wait()
     loads[5].wait()
-
-    slot_row = lax.broadcasted_iota(jnp.int32, (BLK, CW), 0)
-    key_row = slot_head(slot_row // sub) * sub + lax.rem(slot_row, sub)
-    col = lax.broadcasted_iota(jnp.int32, (BLK, CW), 1)
-
-    def halves(a):
-        return a.reshape(BLK // 8, 8, CW)
-
-    def scores(c, _):
-        q_c = q_buf[pl.ds(pl.multiple_of(c * CW, CW), CW), :]
-        top = jnp.full((8, CW), NEG, F32)
-        for e in range(ENT):
-            raw = dot_nt(ksel[e], q_c) * (FACTOR * LOG2E)
-            if e == 0:
-                seen = key_row <= (col + c * CW) // groups
-            else:
-                seen = key_row < vis_ref[0, e - 1]
-            raw = jnp.where(seen, raw, NEG)
-            s_buf[c, e] = raw
-            top = jnp.maximum(top, jnp.max(halves(raw), axis=0))
-        top = jnp.max(top, axis=0, keepdims=True)
-        total = jnp.zeros((8, CW), F32)
-        for e in range(ENT):
-            expo = jnp.exp2(s_buf[c, e] - top)
-            s_buf[c, e] = expo
-            total = total + jnp.sum(halves(expo), axis=0)
-        delta_buf[c] = jnp.broadcast_to(1.0 / jnp.sum(total, axis=0, keepdims=True), (8, CW))
-        return 0
-
-    lax.fori_loop(0, chunks, scores, 0)
-
-    collect(1, last)
-    collected(1)
-    select_pages(1, vsel, vt_sel)
+    scores(0)
+    collected(1, near)
+    select_pages(1, vsel, 0)
+    transposed(vsel, vt_sel, 0)
+    transposed(ksel, kt_sel, 0)
+    for part in rest:
+        collect(0, part)
+        collect(1, part)
+    collected(0, rest)
+    select_pages(0, ksel, 1)
+    scores(1)
+    collected(1, rest)
+    select_pages(1, vsel, 1)
+    transposed(vsel, vt_sel, 1)
 
     def values(c, _):
-        rows_c = pl.ds(pl.multiple_of(c * CW, CW), CW)
-        g_c = g_buf[rows_c, :]
-        inverse = delta_buf[c][:1]
+        g_c = g_buf[lanes(c), :]
+        top = jnp.maximum(top_buf[c, 0], top_buf[c, 1])
+        scale = [jnp.exp2(top_buf[c, h] - top) for h in range(2)]
+        inverse = 1.0 / (sum_buf[c, 0] * scale[0] + sum_buf[c, 1] * scale[1])
         out_t = jnp.zeros((HD, CW), F32)
-        for e in range(ENT):
-            w = s_buf[c, e] * inverse
-            s_buf[c, e] = w
-            w_b = w.astype(BF16)
-            out_t = out_t + dot(vt_sel[:, e * BLK:(e + 1) * BLK], w_b)
-            acc[1, e] += dot(w_b, g_c)
+        for h in range(2):
+            factor = (scale[h] * inverse)[:1]
+            for e in range(ENT):
+                w = s_buf[c, h, e] * factor
+                s_buf[c, h, e] = w
+                ds_buf[c, h, e * hb:(e + 1) * hb, :] = w.astype(BF16)
+            w_b = ds_buf[c, h]
+            acc[1, h, :ENT] += dot(w_b, g_c).reshape(ENT, hb, HD)
+            out_t = out_t + dot(vt_sel[h], w_b)
         out_b = out_t.astype(BF16)
-        att_ref[rows_c, :] = out_b.T
+        att_ref[lanes(c), :] = out_b.T
         delta = jnp.sum(out_b.astype(F32) * gt_buf[c].astype(F32), axis=0, keepdims=True)
         delta_buf[c] = jnp.broadcast_to(delta, (8, CW))
         return 0
@@ -290,8 +313,7 @@
     lax.fori_loop(0, chunks, values, 0)
 
     def slot_sum(t, h, page):
-        part = pl.ds(h * hb, hb)
-        return acc[t, slot_of[0, page], part] + acc[t, slot_of[1, page], part]
+        return acc[t, h, slot_of[0, page]] + acc[t, h, slot_of[1, page]]
 
     def partner_send(t, h, a):
         return remote(dsend.at[t, h, a], prec.at[t, h, a], dd_send.at[0], dd_recv.at[t, h, a], partner, z)
@@ -304,18 +326,17 @@
         to = spot(t, h, 0, b) * 2 + core
         return remote(ssend.at[t, h, b], srec.at[t, h, b], r2_send.at[0], r2_recv.at[t, h], to, z)
 
-    def to_partner(t):
-        for h in (1, 0):
-            for a in far_first(size_a(t, h)) + [0]:
-                for b in range(size_b(t, h)):
-                    dsend[t, h, a, b] = slot_sum(t, h, spot(t, h, a, b) * 2 + (1 - core)).astype(BF16)
-                partner_send(t, h, a).start()
+    def to_partner(t, h):
+        for a in far_first(size_a(t, h)) + [0]:
+            for b in range(size_b(t, h)):
+                dsend[t, h, a, b] = slot_sum(t, h, spot(t, h, a, b) * 2 + (1 - core)).astype(BF16)
+            partner_send(t, h, a).start()
 
     def mine(t, h, a, b):
         return slot_sum(t, h, spot(t, h, a, b) * 2 + core) + prec[t, h, a, b].astype(F32)
 
-    def first_step(t, h):
-        for a in far_first(size_a(t, h)):
+    def first_step(t, h, lo=0, hi=None):
+        for a in far_first(size_a(t, h))[lo:hi]:
             partner_send(t, h, a).wait_recv()
             for b in range(size_b(t, h)):
                 rsend[t, h, a, b] = mine(t, h, a, b).astype(BF16)
@@ -340,7 +361,7 @@
         return remote(fin.at[t, j], zrec.at[t, back], zb_send.at[0], zb_recv.at[t], seq, lax.rem(z + rel[j], nz))
 
     def finish(t, h):
-        total = acc[t, 0, h * hb:(h + 1) * hb] + gathered(t, h, 0)
+        total = acc[t, h, 0] + gathered(t, h, 0)
         here = srec.at[t, h, pl.ds(1, size_b(t, h) - 1)]
         remote(here, here, r2_send.at[0], r2_recv.at[t, h], partner, z).wait_recv()
         for b in range(1, size_b(t, h)):
@@ -359,39 +380,43 @@
         remote(here, here, zb_send.at[0], zb_recv.at[t], seq, lax.rem(z + 1, nz)).wait_recv()
         out_ref[...] = dot(from_slots, zrec[t].reshape(BLK, HD)).astype(BF16)
 
-    def grads(c, _):
-        rows_c = pl.ds(pl.multiple_of(c * CW, CW), CW)
-        g_c = g_buf[rows_c, :]
-        q_c = q_buf[rows_c, :]
-        delta = delta_buf[c][:1]
-        for e in range(ENT):
-            ds = (s_buf[c, e] * (dot_nt(vsel[e], g_c) - delta)).astype(BF16)
-            ds_buf[c, e * BLK:(e + 1) * BLK, :] = ds
-            acc[0, e] += dot(ds, q_c)
+    def grads(h):
+        def step(c, _):
+            g_c = g_buf[lanes(c), :]
+            delta = delta_buf[c][:1]
+            for e in range(ENT):
+                part = pl.ds(e * hb, hb)
+                ds_buf[c, h, part] = (s_buf[c, h, e] * (dot_nt(vsel[h, part], g_c) - delta)).astype(BF16)
+            acc[0, h, :ENT] += dot(ds_buf[c, h], q_buf[lanes(c), :]).reshape(ENT, hb, HD)
+            return 0
+
+        lax.fori_loop(0, chunks, step, 0)
+
+    def query_grads(c, _):
+        dq_t = dot(kt_sel[0], ds_buf[c, 0]) + dot(kt_sel[1], ds_buf[c, 1])
+        qg_ref[lanes(c), :] = (dq_t * FACTOR).T.astype(BF16)
         return 0
 
-    def query_grads(c, _):
-        rows_c = pl.ds(pl.multiple_of(c * CW, CW), CW)
-        dq_t = dot(kt_sel[...], ds_buf[c])
-        qg_ref[rows_c, :] = (dq_t * FACTOR).T.astype(BF16)
-        return 0
-
-    to_partner(1)
-    lax.fori_loop(0, chunks // 2, grads, 0)
+    to_partner(1, 1)
+    to_partner(1, 0)
+    grads(1)
+    to_partner(0, 1)
     first_step(1, 1)
-    first_step(1, 0)
-    lax.fori_loop(chunks // 2, chunks, grads, 0)
-    to_partner(0)
+    first_step(1, 0, 0, 1)
+    grads(0)
+    to_partner(0, 0)
+    first_step(0, 1)
+    first_step(1, 0, 1)
+    transposed(ksel, kt_sel, 1)
+    first_step(0, 0)
     lax.fori_loop(0, chunks, query_grads, 0)
     second_step(1, 1)
+    second_step(0, 1)
     second_step(1, 0)
-    first_step(0, 1)
-    first_step(0, 0)
+    second_step(0, 0)
     finish(1, 1)
+    finish(0, 1)
     finish(1, 0)
-    second_step(0, 1)
-    second_step(0, 0)
-    finish(0, 1)
     finish(0, 0)
     result(1, vg_ref)
     result(0, kg_ref)
@@ -406,9 +431,9 @@
     sent(ssend.at[:, :, pl.ds(1, nx - 1)], r2_send.at[0])
     sent(fin.at[:, pl.ds(1, nz - 1)], zb_send.at[0])
     for t in range(2):
-        sent(pages[t].at[0, pl.ds(0, nx - 1), 0], la_send.at[t])
-        sent(pages[t].at[pl.ds(0, ny - 1), :, 0], pa_send.at[t])
-        sent(pages[t].at[:, :, 0], fw_send.at[t])
+        sent(pages[t][0].at[pl.ds(0, nx - 1), pl.ds(0, 2), 0], la_send.at[t])
+        sent(pages[t][0].at[pl.ds(0, ny - 1)], pa_send.at[t])
+        sent(pages[t][0], fw_send.at[t])
 
 
 def emit(*refs):
@@ -445,16 +470,20 @@
             pltpu.VMEM((rows, HD), BF16),
             pltpu.VMEM((chunks, HD, CW), BF16),
             pltpu.VMEM((chunks, 8, CW), F32),
+            pltpu.VMEM((chunks, 2, 8, CW), F32),
+            pltpu.VMEM((chunks, 2, 8, CW), F32),
             pltpu.VMEM((2, nz, sub, HD), BF16),
-            pltpu.VMEM((ny, nx, 2, nz, sub, HD), BF16),
-            pltpu.VMEM((ny, nx, 2, nz, sub, HD), BF16),
-            pltpu.VMEM((ENT, BLK, HD), BF16),
-            pltpu.VMEM((ENT, BLK, HD), BF16),
-            pltpu.VMEM((HD, ENT * BLK), BF16),
-            pltpu.VMEM((HD, ENT * BLK), BF16),
-            pltpu.VMEM((chunks, ENT, BLK, CW), F32),
-            pltpu.VMEM((chunks, ENT * BLK, CW), BF16),
-            pltpu.VMEM((2, ENT + 1, BLK, HD), F32),
+            pltpu.VMEM((ny, nx, 2, nz // 2, sub, HD), BF16),
+            pltpu.VMEM((ny, nx, 2, nz // 2, sub, HD), BF16),
+            pltpu.VMEM((ny, nx, 2, nz // 2, sub, HD), BF16),
+            pltpu.VMEM((ny, nx, 2, nz // 2, sub, HD), BF16),
+            pltpu.VMEM((2, ENT * hb, HD), BF16),
+            pltpu.VMEM((2, ENT * hb, HD), BF16),
+            pltpu.VMEM((2, HD, ENT * hb), BF16),
+            pltpu.VMEM((2, HD, ENT * hb), BF16),
+            pltpu.VMEM((chunks, 2, ENT, hb, CW), F32),
+            pltpu.VMEM((chunks, 2, ENT * hb, CW), BF16),
+            pltpu.VMEM((2, 2, ENT + 1, hb, HD), F32),
             pltpu.SMEM((1, FORKS), jnp.int32),
             pltpu.SMEM((1, FORKS), jnp.int32),
             pltpu.SMEM((2, 2 * nc), jnp.int32),
@@ -467,10 +496,10 @@
             pltpu.VMEM((2, nz, sub, HD), BF16),
             pltpu.VMEM((2, nz, sub, HD), BF16),
             dma((6,)),
-            dma((1,)), dma((2, 4)),
-            dma((2,)), dma((2, 4)),
-            dma((2,)), dma((2, 4)),
-            dma((2,)), dma((2, 4)),
+            dma((1,)), dma((2, 5)),
+            dma((2,)), dma((2, 5)),
+            dma((2,)), dma((2, 5)),
+            dma((2,)), dma((2, 5)),
             dma((1,)), dma((2, 2, nm)),
             dma((1,)), dma((2, 2)),
             dma((1,)), dma((2, 2)),

time: 51.5 us -> 51.7 us (level)
  no operation moved by 1% of the time
where the time goes in v4:
time: 51.7 us; the launch traced here: 51.5 us
  Pallas kernels  50.8 us (98%)
  between operations  0.64 us (1%)
    pallas_call x1, Pallas kernels, per_device(): pl.pallas_call(functools.partial(kernel, nx, ny, nz, groups), out_shape=t...  50 us

profile of v4, /device:TPU:1, one launch (start us, length us, event | category | flops | bytes accessed | tf_op | source)
XLA Modules:
  0.0 51.5 jit_solution(2794856792515264308)
XLA Ops:
  0.6 50.0 %shard_map.93 = (bf16[1024,128]{1,0:T(8,128)(2,1)S(1)}, bf16[1024,128]{1,0:T(8,128)(2,1)S(1)}, bf16[128,128]{1,0:T(8,128)(2,1)S(1)}, bf16[128,128]{1,0:T(8,128)(2,1)S(1)}) custom-call(s32[1,8]{1,0:T(1,128)} %fork_hbm.1, s32[1,8]{1,0:T(1,128)} %vis_hbm.1, bf16[128,128]{1,0:T(8,128)(2,1)} %bitcast.10, bf16[128,128]{1,0:T(8,128)(2,1)} %bitcast.11, ...), custom_call_target="tpu_custom_call" | custom-call | tf_op jit(solution)/shard_map/pallas_call | solution.py:462
  50.6 0.8 %shard_map.94 = (bf16[1024,128]{1,0:T(8,128)(2,1)}, bf16[1024,128]{1,0:T(8,128)(2,1)}, bf16[128,128]{1,0:T(8,128)(2,1)}, bf16[128,128]{1,0:T(8,128)(2,1)}) custom-call(bf16[1024,128]{1,0:T(8,128)(2,1)S(1)} %get-tuple-element.12.refs_0_, bf16[1024,128]{1,0:T(8,128)(2,1)S(1)} %get-tuple-element.13.refs_1_, bf16[128,128]{1,0:T(8,128)(2,1)S(1)} %get-tuple-element.14.refs_2_, ...), custom_call_target="tpu_custom_call" | custom-call | tf_op jit(solution)/shard_map/pallas_call | solution.py:516

commit v5 on v4

--- a/solution.py
+++ b/solution.py
@@ -69,7 +69,7 @@
 
     rel = [(j + 1) // 2 if j % 2 else (nz - j // 2) % nz for j in range(nz)]
     slot_at = {r: j for j, r in enumerate(rel)}
-    bounds = [0, 1, 3, 4, 5, 8] if nz == 8 else [0, 1, nz]
+    bounds = [0, 1, 4, 8] if nz == 8 else [0, 1, nz]
     parts = list(zip(bounds[:-1], bounds[1:]))
     part_of = [p for p, (lo, hi) in enumerate(parts) for _ in range(lo, hi)]
 
@@ -167,8 +167,10 @@
 
     def send_part(part):
         for t in range(2):
-            if part:
-                here = own_part(t, part)
+            lo, hi = parts[part]
+            first = max(lo, 1)
+            if first < hi:
+                here = pages[t][lo // hz].at[y, x, core, pl.ds(first % hz, hi - first)]
                 remote(here, here, z_send.at[0], z_recv.at[t, part], seq, lax.rem(z + 1, nz)).wait_recv()
             for d in far_first(size_a(t, part)):
                 line_send(t, part, d).start()

time: 51.7 us -> 50.2 us (0.971)
  Pallas kernels: 50.8 us -> 49.4 us
    pallas_call x1, Pallas kernels: 50 us -> 48.6 us  [per_device(): pl.pallas_call(functools.partial(kernel, nx, ny, nz, groups), out_shape=t...]
where the time goes in v5:
time: 50.2 us; the launch traced here: 50.1 us
  Pallas kernels  49.4 us (98%)
  between operations  0.64 us (1%)
    pallas_call x1, Pallas kernels, per_device(): pl.pallas_call(functools.partial(kernel, nx, ny, nz, groups), out_shape=t...  48.6 us

profile of v5, /device:TPU:1, one launch (start us, length us, event | category | flops | bytes accessed | tf_op | source)
XLA Modules:
  0.0 50.1 jit_solution(2221539889359699187)
XLA Ops:
  0.6 48.6 %shard_map.93 = (bf16[1024,128]{1,0:T(8,128)(2,1)S(1)}, bf16[1024,128]{1,0:T(8,128)(2,1)S(1)}, bf16[128,128]{1,0:T(8,128)(2,1)S(1)}, bf16[128,128]{1,0:T(8,128)(2,1)S(1)}) custom-call(s32[1,8]{1,0:T(1,128)} %fork_hbm.1, s32[1,8]{1,0:T(1,128)} %vis_hbm.1, bf16[128,128]{1,0:T(8,128)(2,1)} %bitcast.10, bf16[128,128]{1,0:T(8,128)(2,1)} %bitcast.11, ...), custom_call_target="tpu_custom_call" | custom-call | tf_op jit(solution)/shard_map/pallas_call | solution.py:464
  49.2 0.8 %shard_map.94 = (bf16[1024,128]{1,0:T(8,128)(2,1)}, bf16[1024,128]{1,0:T(8,128)(2,1)}, bf16[128,128]{1,0:T(8,128)(2,1)}, bf16[128,128]{1,0:T(8,128)(2,1)}) custom-call(bf16[1024,128]{1,0:T(8,128)(2,1)S(1)} %get-tuple-element.12.refs_0_, bf16[1024,128]{1,0:T(8,128)(2,1)S(1)} %get-tuple-element.13.refs_1_, bf16[128,128]{1,0:T(8,128)(2,1)S(1)} %get-tuple-element.14.refs_2_, ...), custom_call_target="tpu_custom_call" | custom-call | tf_op jit(solution)/shard_map/pallas_call | solution.py:518

commit v6 on v5

--- a/solution.py
+++ b/solution.py
@@ -287,32 +287,26 @@
     collected(0, rest)
     select_pages(0, ksel, 1)
     scores(1)
-    collected(1, rest)
-    select_pages(1, vsel, 1)
-    transposed(vsel, vt_sel, 1)
-
-    def values(c, _):
+    def weigh(c, _):
         g_c = g_buf[lanes(c), :]
         top = jnp.maximum(top_buf[c, 0], top_buf[c, 1])
         scale = [jnp.exp2(top_buf[c, h] - top) for h in range(2)]
         inverse = 1.0 / (sum_buf[c, 0] * scale[0] + sum_buf[c, 1] * scale[1])
-        out_t = jnp.zeros((HD, CW), F32)
         for h in range(2):
             factor = (scale[h] * inverse)[:1]
             for e in range(ENT):
                 w = s_buf[c, h, e] * factor
                 s_buf[c, h, e] = w
                 ds_buf[c, h, e * hb:(e + 1) * hb, :] = w.astype(BF16)
-            w_b = ds_buf[c, h]
-            acc[1, h, :ENT] += dot(w_b, g_c).reshape(ENT, hb, HD)
-            out_t = out_t + dot(vt_sel[h], w_b)
-        out_b = out_t.astype(BF16)
+            acc[1, h, :ENT] += dot(ds_buf[c, h], g_c).reshape(ENT, hb, HD)
+        return 0
+
+    def attend(c, _):
+        out_b = (dot(vt_sel[0], ds_buf[c, 0]) + dot(vt_sel[1], ds_buf[c, 1])).astype(BF16)
         att_ref[lanes(c), :] = out_b.T
         delta = jnp.sum(out_b.astype(F32) * gt_buf[c].astype(F32), axis=0, keepdims=True)
         delta_buf[c] = jnp.broadcast_to(delta, (8, CW))
         return 0
-
-    lax.fori_loop(0, chunks, values, 0)
 
     def slot_sum(t, h, page):
         return acc[t, h, slot_of[0, page]] + acc[t, h, slot_of[1, page]]
@@ -399,12 +393,17 @@
         qg_ref[lanes(c), :] = (dq_t * FACTOR).T.astype(BF16)
         return 0
 
+    lax.fori_loop(0, chunks, weigh, 0)
     to_partner(1, 1)
     to_partner(1, 0)
+    collected(1, rest)
+    select_pages(1, vsel, 1)
+    transposed(vsel, vt_sel, 1)
+    lax.fori_loop(0, chunks, attend, 0)
+    first_step(1, 1)
+    first_step(1, 0, 0, 1)
     grads(1)
     to_partner(0, 1)
-    first_step(1, 1)
-    first_step(1, 0, 0, 1)
     grads(0)
     to_partner(0, 0)
     first_step(0, 1)

time: 50.2 us -> 50.8 us (1.012)
  Pallas kernels: 49.4 us -> 50 us
    pallas_call x1, Pallas kernels: 48.6 us -> 49.2 us  [per_device(): pl.pallas_call(functools.partial(kernel, nx, ny, nz, groups), out_shape=t...]
where the time goes in v6:
time: 50.8 us; the launch traced here: 50.7 us
  Pallas kernels  50 us (98%)
  between operations  0.64 us (1%)
    pallas_call x1, Pallas kernels, per_device(): pl.pallas_call(functools.partial(kernel, nx, ny, nz, groups), out_shape=t...  49.2 us

profile of v6, /device:TPU:1, one launch (start us, length us, event | category | flops | bytes accessed | tf_op | source)
XLA Modules:
  0.0 50.7 jit_solution(17285730842435127181)
XLA Ops:
  0.6 49.2 %shard_map.93 = (bf16[1024,128]{1,0:T(8,128)(2,1)S(1)}, bf16[1024,128]{1,0:T(8,128)(2,1)S(1)}, bf16[128,128]{1,0:T(8,128)(2,1)S(1)}, bf16[128,128]{1,0:T(8,128)(2,1)S(1)}) custom-call(s32[1,8]{1,0:T(1,128)} %fork_hbm.1, s32[1,8]{1,0:T(1,128)} %vis_hbm.1, bf16[128,128]{1,0:T(8,128)(2,1)} %bitcast.10, bf16[128,128]{1,0:T(8,128)(2,1)} %bitcast.11, ...), custom_call_target="tpu_custom_call" | custom-call | tf_op jit(solution)/shard_map/pallas_call | solution.py:463
  49.8 0.8 %shard_map.94 = (bf16[1024,128]{1,0:T(8,128)(2,1)}, bf16[1024,128]{1,0:T(8,128)(2,1)}, bf16[128,128]{1,0:T(8,128)(2,1)}, bf16[128,128]{1,0:T(8,128)(2,1)}) custom-call(bf16[1024,128]{1,0:T(8,128)(2,1)S(1)} %get-tuple-element.12.refs_0_, bf16[1024,128]{1,0:T(8,128)(2,1)S(1)} %get-tuple-element.13.refs_1_, bf16[128,128]{1,0:T(8,128)(2,1)S(1)} %get-tuple-element.14.refs_2_, ...), custom_call_target="tpu_custom_call" | custom-call | tf_op jit(solution)/shard_map/pallas_call | solution.py:517

commit v7 on v5

--- a/solution.py
+++ b/solution.py
@@ -200,10 +200,8 @@
 
     for part in range(1, len(parts)):
         send_part(part)
-        if part > 1:
-            relay(part - 2)
-    for part in range(max(0, len(parts) - 2), len(parts)):
-        relay(part)
+        relay(part - 1)
+    relay(len(parts) - 1)
     loads[4].wait()
     lax.fori_loop(0, 2 * nc, entry_slots, 0)
     for t in range(2):
@@ -277,13 +275,13 @@
     loads[3].wait()
     loads[5].wait()
     scores(0)
+    for part in rest:
+        collect(0, part)
+        collect(1, part)
     collected(1, near)
     select_pages(1, vsel, 0)
     transposed(vsel, vt_sel, 0)
     transposed(ksel, kt_sel, 0)
-    for part in rest:
-        collect(0, part)
-        collect(1, part)
     collected(0, rest)
     select_pages(0, ksel, 1)
     scores(1)
@@ -404,21 +402,20 @@
     grads(1)
     to_partner(0, 1)
     first_step(1, 1)
-    first_step(1, 0, 0, 1)
+    first_step(1, 0)
     grads(0)
     to_partner(0, 0)
     first_step(0, 1)
-    first_step(1, 0, 1)
     transposed(ksel, kt_sel, 1)
     first_step(0, 0)
     lax.fori_loop(0, chunks, query_grads, 0)
     second_step(1, 1)
+    second_step(1, 0)
     second_step(0, 1)
-    second_step(1, 0)
+    finish(1, 1)
     second_step(0, 0)
-    finish(1, 1)
+    finish(1, 0)
     finish(0, 1)
-    finish(1, 0)
     finish(0, 0)
     result(1, vg_ref)
     result(0, kg_ref)

time: 50.2 us -> 49.3 us (0.982)
  Pallas kernels: 49.4 us -> 48.5 us
    pallas_call x1, Pallas kernels: 48.6 us -> 47.7 us  [per_device(): pl.pallas_call(functools.partial(kernel, nx, ny, nz, groups), out_shape=t...]
where the time goes in v7:
time: 49.3 us; the launch traced here: 49.1 us
  Pallas kernels  48.5 us (98%)
  between operations  0.64 us (1%)
    pallas_call x1, Pallas kernels, per_device(): pl.pallas_call(functools.partial(kernel, nx, ny, nz, groups), out_shape=t...  47.7 us

profile of v7, /device:TPU:1, one launch (start us, length us, event | category | flops | bytes accessed | tf_op | source)
XLA Modules:
  0.0 49.1 jit_solution(814989149472424422)
XLA Ops:
  0.6 47.7 %shard_map.93 = (bf16[1024,128]{1,0:T(8,128)(2,1)S(1)}, bf16[1024,128]{1,0:T(8,128)(2,1)S(1)}, bf16[128,128]{1,0:T(8,128)(2,1)S(1)}, bf16[128,128]{1,0:T(8,128)(2,1)S(1)}) custom-call(s32[1,8]{1,0:T(1,128)} %fork_hbm.1, s32[1,8]{1,0:T(1,128)} %vis_hbm.1, bf16[128,128]{1,0:T(8,128)(2,1)} %bitcast.10, bf16[128,128]{1,0:T(8,128)(2,1)} %bitcast.11, ...), custom_call_target="tpu_custom_call" | custom-call | tf_op jit(solution)/shard_map/pallas_call | solution.py:461
  48.3 0.8 %shard_map.94 = (bf16[1024,128]{1,0:T(8,128)(2,1)}, bf16[1024,128]{1,0:T(8,128)(2,1)}, bf16[128,128]{1,0:T(8,128)(2,1)}, bf16[128,128]{1,0:T(8,128)(2,1)}) custom-call(bf16[1024,128]{1,0:T(8,128)(2,1)S(1)} %get-tuple-element.12.refs_0_, bf16[1024,128]{1,0:T(8,128)(2,1)S(1)} %get-tuple-element.13.refs_1_, bf16[128,128]{1,0:T(8,128)(2,1)S(1)} %get-tuple-element.14.refs_2_, ...), custom_call_target="tpu_custom_call" | custom-call | tf_op jit(solution)/shard_map/pallas_call | solution.py:515
